TPU v7x, 128 devices: a whole 4x4x4 slice. The times are simulated.
128 devices in a mesh: node: 8 (over z, core), local: 16 (over y, x).
Axes of the slice: x: 4, y: 4, z: 4, core: 2. Of those that a mesh axis runs over, the one named last changes fastest.
Arguments:
- tokens: bfloat16 [2048, 7168], P(('node', 'local')), may hold values from -6 to 6
- grad_out: bfloat16 [2048, 7168], P(('node', 'local')), may hold values from -6 to 6
- gates: bfloat16 [2048, 3], P(('node', 'local')), may hold values from 0.19921875 to 1
- expert_ids: int32 [2048, 3], P(('node', 'local')), may hold values from 0 to 15, as said below
- w_gate: bfloat16 [8, 7168, 2048], P('node', None, 'local'), may hold values from -0.0625 to 0.0625
- w_up: bfloat16 [8, 7168, 2048], P('node', None, 'local'), may hold values from -0.0625 to 0.0625
- w_down: bfloat16 [8, 7168, 2048], P('node', None, 'local'), may hold values from -0.1875 to 0.1875
- s_gate: bfloat16 [7168, 2048], P(None, 'local'), may hold values from -0.0625 to 0.0625
- s_up: bfloat16 [7168, 2048], P(None, 'local'), may hold values from -0.0625 to 0.0625
- s_down: bfloat16 [7168, 2048], P(None, 'local'), may hold values from -0.125 to 0.125
Outputs:
- dx: bfloat16 [2048, 7168], P(('node', 'local'))
- dgates: float32 [2048, 3], P(('node', 'local'))
- d_w_gate: bfloat16 [8, 7168, 2048], P('node', None, 'local')
- d_w_up: bfloat16 [8, 7168, 2048], P('node', None, 'local')
- d_w_down: bfloat16 [8, 7168, 2048], P('node', None, 'local')
- d_s_gate: bfloat16 [7168, 2048], P('node', 'local')
- d_s_up: bfloat16 [7168, 2048], P('node', 'local')
- d_s_down: bfloat16 [7168, 2048], P('node', 'local')
Inputs may be any that keep to these rules, and one draw needn't show every extreme that they name: `expert_ids`: each token names both experts of one node and one expert of a second node. Of the tokens of one device exactly 4 name experts of each node and at most 4 name any one expert; for every node one of its experts is named by exactly 4 tokens of every device.
All inputs are finite; a program needn't handle non-finite values.
Results may differ from a plain program's by a relative error of at most 0.014.
Values may be sent and summed in bfloat16 or wider, within the bound.
A program may use at most 192 MiB of HBM per device.

v0:
```python
import jax
import jax.numpy as jnp
from jax import lax
from jax.sharding import PartitionSpec as P

E_NODE = 2


precise = lax.Precision.HIGHEST


def split_up(value, dim, devices):
    before, after = (value.shape[:dim], value.shape[dim + 1 :])
    return jnp.moveaxis(value.reshape(*before, devices, -1, *after), dim, 0)


def summed_on_arrival(value, axis, dim):
    tiles = split_up(value, dim, lax.axis_size(axis))
    arrived = lax.all_to_all(tiles, axis, split_axis=0, concat_axis=0, tiled=True)
    return arrived.astype(jnp.float32).sum(axis=0)


def in_one_piece(arrays, axis, split_dim, concat_dim, along):
    columns = [a.reshape(*a.shape[:along], -1) for a in arrays]
    both = jnp.concatenate(columns, axis=along)
    out, at, gathered = (
        lax.all_to_all(both, axis, split_axis=split_dim, concat_axis=concat_dim, tiled=True),
        0,
        [],
    )
    for a, column in zip(arrays, columns):
        piece = out[..., at : at + column.shape[along]]
        gathered.append(piece.reshape(*piece.shape[:along], *a.shape[along:]))
        at += column.shape[along]
    return tuple(gathered)


def silu_parts(pre_gate):
    sig = jax.nn.sigmoid(pre_gate)
    return (pre_gate * sig, sig * (1.0 + pre_gate * (1.0 - sig)))


def contract_first(left, right):
    return lax.dot_general(
        left, right, (((0,), (0,)), ((), ())), preferred_element_type=jnp.float32
    )


def contract_last(left, right):
    return lax.dot_general(
        left, right, (((1,), (1,)), ((), ())), preferred_element_type=jnp.float32
    )


def ffn_backward(rows_in, rows_grad, weight, gate_w, up_w, down_w):
    pre_gate = jnp.dot(rows_in, gate_w, preferred_element_type=jnp.float32)
    pre_up = jnp.dot(rows_in, up_w, preferred_element_type=jnp.float32)
    activ, slope = silu_parts(pre_gate)
    hidden = activ * pre_up
    upstream = jnp.dot(rows_grad, down_w, preferred_element_type=jnp.float32)
    scaled = weight * upstream
    grad_up = (scaled * activ).astype(jnp.bfloat16)
    grad_gate = (scaled * pre_up * slope).astype(jnp.bfloat16)
    weighted = (weight * hidden).astype(jnp.bfloat16)
    return (grad_gate, grad_up, weighted, hidden * upstream)


def expert_work(rows_in, rows_grad, weight, gate_w, up_w, down_w):
    grad_gate, grad_up, weighted, product = ffn_backward(
        rows_in, rows_grad, weight, gate_w, up_w, down_w
    )
    partial_value = (contract_last(grad_gate, gate_w) + contract_last(grad_up, up_w)).astype(
        jnp.bfloat16
    )
    score = jnp.sum(product, axis=1).astype(jnp.bfloat16)
    grads = (
        contract_first(rows_in, grad_gate),
        contract_first(rows_in, grad_up),
        contract_first(rows_grad, weighted),
    )
    return (partial_value, score, grads)


def shared_part(tokens, grad_out, s_gate, s_up, s_down):
    rows_in, rows_grad = (
        lax.all_gather(tokens, "local", axis=0, tiled=True),
        lax.all_gather(grad_out, "local", axis=0, tiled=True),
    )
    unit_weight = jnp.ones((rows_in.shape[0], 1), jnp.float32)
    grad_gate, grad_up, weighted, product = ffn_backward(
        rows_in, rows_grad, unit_weight, s_gate, s_up, s_down
    )
    dx_shared = summed_on_arrival(
        (contract_last(grad_gate, s_gate) + contract_last(grad_up, s_up)).astype(jnp.bfloat16),
        "local",
        0,
    )
    units = s_gate.shape[1]
    shares = lax.psum_scatter(
        jnp.concatenate(
            [
                contract_first(rows_in, grad_gate),
                contract_first(rows_in, grad_up),
                contract_first(rows_grad, weighted),
            ],
            axis=1,
        ).astype(jnp.bfloat16),
        "node",
        scatter_dimension=0,
        tiled=True,
    ).astype(jnp.float32)
    shared_grads = (
        shares[:, :units].astype(jnp.bfloat16),
        shares[:, units : 2 * units].astype(jnp.bfloat16),
        shares[:, 2 * units :].astype(jnp.bfloat16),
    )
    return (dx_shared, shared_grads)


def routed_part(tokens, grad_out, gates, expert_ids, gate_w, up_w, down_w):
    tokens_here = tokens.shape[0]
    width = tokens.shape[1]
    node_count = lax.axis_size("node")
    local_count = lax.axis_size("local")
    group_size = local_count // E_NODE
    capacity = 2 * tokens_here // node_count
    expert_count = E_NODE * node_count
    slots = jnp.arange(capacity, dtype=jnp.int32)
    chosen = expert_ids[:, :, None] == jnp.arange(expert_count, dtype=jnp.int32)[None, None, :]
    member = jnp.any(chosen, axis=1)
    weight = jnp.sum(jnp.where(chosen, gates.astype(jnp.float32)[:, :, None], 0.0), axis=1)
    ranking = jnp.cumsum(member.astype(jnp.int32), axis=0) - 1
    slot_pick = member[:, :, None] & (ranking[:, :, None] == slots[None, None, :])
    pick_float = slot_pick.astype(jnp.float32)
    slot_gate = jnp.einsum("tes,te->es", pick_float, weight, precision=precise)
    pick_rows = slot_pick.astype(jnp.bfloat16)
    send_in = jnp.einsum(
        "tes,td->esd", pick_rows, tokens, preferred_element_type=jnp.float32
    ).astype(jnp.bfloat16)
    send_grad = jnp.einsum(
        "tes,td->esd", pick_rows, grad_out, preferred_element_type=jnp.float32
    ).astype(jnp.bfloat16)

    def spread(values):
        shaped = values.reshape((node_count, E_NODE, 1) + values.shape[1:])
        wide = jnp.broadcast_to(shaped, (node_count, E_NODE, group_size) + values.shape[1:])
        return wide.reshape((node_count * local_count,) + values.shape[1:])

    got_in, got_grad, got_gate = in_one_piece(
        (spread(send_in), spread(send_grad), spread(slot_gate.astype(jnp.bfloat16))),
        ("node", "local"),
        0,
        0,
        2,
    )
    partial_value, score, grads = expert_work(
        got_in.reshape(-1, width),
        got_grad.reshape(-1, width),
        got_gate.reshape(-1, 1).astype(jnp.float32),
        gate_w,
        up_w,
        down_w,
    )
    back_dx, back_score = (
        lax.all_to_all(
            partial_value.reshape(got_in.shape),
            ("node", "local"),
            split_axis=0,
            concat_axis=0,
            tiled=True,
        ),
        lax.all_to_all(
            score.reshape(got_gate.shape),
            ("node", "local"),
            split_axis=0,
            concat_axis=0,
            tiled=True,
        ),
    )
    slot_dx = jnp.sum(
        back_dx.reshape(node_count, E_NODE, group_size, capacity, width).astype(jnp.float32), axis=2
    ).reshape(expert_count, capacity, width)
    slot_score = jnp.sum(
        back_score.reshape(node_count, E_NODE, group_size, capacity).astype(jnp.float32), axis=2
    ).reshape(expert_count, capacity)
    dx_routed = jnp.einsum("tes,esd->td", pick_float, slot_dx, precision=precise)
    token_score = jnp.einsum("tes,es->te", pick_float, slot_score, precision=precise)
    dgates = jnp.sum(jnp.where(chosen, token_score[:, None, :], 0.0), axis=2)
    return (dx_routed, dgates, grads)


def local(tokens, grad_out, gates, expert_ids, w_gate, w_up, w_down, s_gate, s_up, s_down):
    dx_routed, dgates, grads = routed_part(
        tokens, grad_out, gates, expert_ids, w_gate[0], w_up[0], w_down[0]
    )
    dx_shared, shared_grads = shared_part(tokens, grad_out, s_gate, s_up, s_down)
    dx = (dx_routed + dx_shared).astype(jnp.bfloat16)
    expert_grads = tuple((grad.astype(jnp.bfloat16)[None] for grad in grads))
    return (
        dx,
        dgates,
        expert_grads[0],
        expert_grads[1],
        expert_grads[2],
        shared_grads[0],
        shared_grads[1],
        shared_grads[2],
    )


def solution(mesh):
    placed = (
        P(("node", "local"), None),
        P(("node", "local"), None),
        P(("node", "local"), None),
        P(("node", "local"), None),
        P("node", None, "local"),
        P("node", None, "local"),
        P("node", None, "local"),
        P(None, "local"),
        P(None, "local"),
        P(None, "local"),
    )
    return jax.shard_map(
        local,
        mesh=mesh,
        in_specs=placed,
        out_specs=(
            P(("node", "local"), None),
            P(("node", "local"), None),
            P("node", None, "local"),
            P("node", None, "local"),
            P("node", None, "local"),
            P("node", "local"),
            P("node", "local"),
            P("node", "local"),
        ),
        check_vma=False,
    )
```

profile of v0, /device:TPU:11, one launch (start us, length us, event | category | flops | bytes accessed | tf_op | source)
XLA Modules:
  0.0 506.0 jit_solution(10965011893710607387)
XLA Ops:
  15.1 5.2 %broadcast_in_dim.60 = bf16[8,2,8,4,7168]{4,3,2,1,0:T(4,128)(2,1)} broadcast(bf16[8,2,4,7168]{3,2,1,0:T(4,128)(2,1)S(1)} %bitcast.98), dimensions={0,1,3,4} | broadcast | bytes 8257536 | tf_op jit(solution)/shard_map/broadcast_in_dim | solution.py:146
  20.3 5.2 %broadcast_in_dim.62 = bf16[8,2,8,4,7168]{4,3,2,1,0:T(4,128)(2,1)} broadcast(bf16[8,2,4,7168]{3,2,1,0:T(4,128)(2,1)S(1)} %bitcast.97), dimensions={0,1,3,4} | broadcast | bytes 8257536 | tf_op jit(solution)/shard_map/broadcast_in_dim | solution.py:146
  25.5 11.0 %pad_maximum_fusion = bf16[128,4,14337]{2,1,0:T(4,128)(2,1)} fusion(bf16[128,4,1]{2,1,0:T(4,128)(2,1)S(1)} %copy.67, bf16[128,4,7168]{2,1,0:T(4,128)(2,1)} %bitcast.94, bf16[128,4,7168]{2,1,0:T(4,128)(2,1)} %bitcast.93), kind=kLoop, calls=%fused_computation | loop fusion | flops 44043264 | bytes 29362176 | tf_op jit(solution)/shard_map/concatenate | solution.py:25
  36.5 11.2 %all-to-all-start = ((bf16[128,4,14337]{2,1,0:T(4,128)(2,1)}), bf16[128,4,14337]{2,1,0:T(4,128)(2,1)}, u32[]{:S(2)}, u32[]{:S(2)}) async-start(bf16[128,4,14337]{2,1,0:T(4,128)(2,1)} %pad_maximum_fusion), calls=%async_computation | async-start | bytes 29622272 | tf_op jit(solution)/shard_map/all_to_all | solution.py:27
  48.6 75.9 %all-gather.5.cloned.1.call-done = bf16[256,7168]{1,0:T(8,128)(2,1)} async-done(((bf16[16,7168]{1,0:T(8,128)(2,1)}), bf16[256,7168]{1,0:T(8,128)(2,1)}) %all-gather.5.cloned.1.call-update) | async-done | bytes 3670032 | tf_op jit(solution)/shard_map/all_gather | solution.py:86
  124.6 3.9 fusion.44
  130.0 129.1 %all-gather.3.cloned.1.call-done = bf16[256,7168]{1,0:T(8,128)(2,1)} async-done(((bf16[16,7168]{1,0:T(8,128)(2,1)}), bf16[256,7168]{1,0:T(8,128)(2,1)}) %all-gather.3.cloned.1.call-update) | async-done | bytes 3670032 | tf_op jit(solution)/shard_map/all_gather | solution.py:87
  259.1 3.9 multiply_convert_fusion.5
  269.5 8.3 %copy.90 = bf16[7168,384]{1,0:T(8,128)(2,1)} copy(bf16[7168,384]{0,1:T(8,128)(2,1)} %pad_maximum_fusion.1) | data formatting | bytes 11010048
  283.6 6.2 %all-to-all-done = bf16[128,4,14337]{2,1,0:T(4,128)(2,1)} async-done(((bf16[128,4,14337]{2,1,0:T(4,128)(2,1)}), bf16[128,4,14337]{2,1,0:T(4,128)(2,1)}, u32[]{:S(2)}, u32[]{:S(2)}) %all-to-all-start) | async-done | bytes 14681120 | tf_op jit(solution)/shard_map/all_to_all | solution.py:27
  289.8 8.6 %all-to-all-start.2 = ((bf16[16,16,7168]{2,1,0:T(8,128)(2,1)}), bf16[16,16,7168]{2,1,0:T(8,128)(2,1)}, u32[]{:S(2)}, u32[]{:S(2)}) async-start(bf16[16,16,7168]{2,1,0:T(8,128)(2,1)} %bitcast.95), calls=%async_computation.2 | async-start | bytes 7340032 | tf_op jit(solution)/shard_map/all_to_all | solution.py:19
  298.4 15.2 %fusion.41 = (bf16[128,4,7168]{2,1,0:T(4,128)(2,1)}, bf16[128,4,7168]{2,1,0:T(4,128)(2,1)}) fusion(bf16[128,4,14337]{2,1,0:T(4,128)(2,1)} %all-to-all-done), kind=kLoop, calls=%fused_computation.68 | loop fusion | bytes 29360128 | tf_op jit(solution)/shard_map/slice | solution.py:32
  314.8 12.1 %reshape.92 = bf16[512,7168]{1,0:T(8,128)(2,1)} reshape(bf16[128,4,7168]{2,1,0:T(4,128)(2,1)} %get-tuple-element.48) | data formatting | bytes 14680064 | tf_op jit(solution)/shard_map/reshape | solution.py:158
  326.9 12.1 %reshape.93 = bf16[512,7168]{1,0:T(8,128)(2,1)} reshape(bf16[128,4,7168]{2,1,0:T(4,128)(2,1)} %get-tuple-element.49) | data formatting | bytes 14680064 | tf_op jit(solution)/shard_map/reshape | solution.py:157
  339.0 5.8 %fusion.11 = f32[512,128]{0,1:T(8,128)S(1)} fusion(bf16[512,7168]{1,0:T(8,128)(2,1)} %reshape.93, bf16[1,7168,128]{2,1,0:T(8,128)(2,1)S(1)} %copy-done), kind=kOutput, calls=%fused_computation.26 | convolution fusion | flops 939524096 | bytes 9437184 | tf_op jit(solution)/shard_map/dot_general | solution.py:56
  351.8 7.3 %fusion.9 = f32[512,7168]{1,0:T(8,128)} fusion(bf16[512,128]{0,1:T(8,128)(2,1)S(1)} %get-tuple-element.51, bf16[1,7168,128]{2,1,0:T(8,128)(2,1)S(1)} %copy-done), kind=kOutput, calls=%fused_computation.24 | convolution fusion | flops 939524096 | bytes 16646144 | tf_op jit(solution)/shard_map/dot_general | solution.py:50
  359.1 7.5 %all-to-all-start.3 = ((bf16[128,1,4]{2,1,0:T(2,128)(2,1)}), bf16[128,1,4]{2,1,0:T(2,128)(2,1)S(1)}, u32[]{:S(2)}, u32[]{:S(2)}) async-start(bf16[128,1,4]{2,1,0:T(2,128)(2,1)} %convert_element_type.134), calls=%async_computation.3 | async-start | bytes 131072 | tf_op jit(solution)/shard_map/all_to_all | solution.py:172
  366.6 10.7 %add_convert_fusion = bf16[512,7168]{1,0:T(8,128)(2,1)} fusion(f32[512,7168]{1,0:T(8,128)} %fusion.9, bf16[512,128]{0,1:T(8,128)(2,1)S(1)} %get-tuple-element.55, bf16[1,7168,128]{2,1,0:T(8,128)(2,1)} %param.15), kind=kOutput, calls=%fused_computation.2 | convolution fusion | flops 946864128 | bytes 23986176 | tf_op jit(solution)/shard_map/dot_general | solution.py:50
  377.3 12.7 %reshape.94 = bf16[128,4,7168]{2,1,0:T(4,128)(2,1)} reshape(bf16[512,7168]{1,0:T(8,128)(2,1)} %add_convert_fusion) | data formatting | bytes 14680064 | tf_op jit(solution)/shard_map/reshape | solution.py:166
  390.0 10.4 %all-to-all-start.1 = ((bf16[128,4,7168]{2,1,0:T(4,128)(2,1)}), bf16[128,4,7168]{2,1,0:T(4,128)(2,1)}, u32[]{:S(2)}, u32[]{:S(2)}) async-start(bf16[128,4,7168]{2,1,0:T(4,128)(2,1)} %reshape.94), calls=%async_computation.1 | async-start | bytes 14680064 | tf_op jit(solution)/shard_map/all_to_all | solution.py:165
  403.2 6.6 %fusion.1 = bf16[1,7168,128]{2,1,0:T(8,128)(2,1)} fusion(bf16[512,7168]{1,0:T(8,128)(2,1)} %reshape.93, bf16[512,128]{0,1:T(8,128)(2,1)S(1)} %get-tuple-element.51), kind=kOutput, calls=%fused_computation.11 | convolution fusion | flops 940441600 | bytes 9306112 | tf_op jit(solution)/shard_map/dot_general | solution.py:44
  413.2 3.4 fusion.3
  419.6 69.9 %all-to-all-done.1 = bf16[128,4,7168]{2,1,0:T(4,128)(2,1)} async-done(((bf16[128,4,7168]{2,1,0:T(4,128)(2,1)}), bf16[128,4,7168]{2,1,0:T(4,128)(2,1)}, u32[]{:S(2)}, u32[]{:S(2)}) %all-to-all-start.1) | async-done | bytes 7340064 | tf_op jit(solution)/shard_map/all_to_all | solution.py:165
  489.5 6.8 %convert_reduce_fusion = f32[8,2,4,7168]{3,2,1,0:T(4,128)S(1)} fusion(bf16[128,4,7168]{2,1,0:T(4,128)(2,1)} %all-to-all-done.1), kind=kLoop, calls=%fused_computation.1 | loop fusion | flops 6881280 | bytes 9175040 | tf_op jit(solution)/shard_map/reduce_sum | solution.py:180
  (78 shorter events, 42.5 us)
Async XLA Ops:
  7.2 331.8 %copy-start = (bf16[1,7168,128]{2,1,0:T(8,128)(2,1)S(1)}, bf16[1,7168,128]{2,1,0:T(8,128)(2,1)}, u32[]{:S(2)}) copy-start(bf16[1,7168,128]{2,1,0:T(8,128)(2,1)} %param.14) | copy-start | bytes 5505028
  7.2 117.4 %all-gather.5.cloned.1.call-start = ((), (), s32[]{:S(2)}) async-start(), calls=%async_computation.6 | async-start | bytes 3899392 | tf_op jit(solution)/shard_map/all_gather | solution.py:86
  36.5 253.3 %all-to-all-start = ((bf16[128,4,14337]{2,1,0:T(4,128)(2,1)}), bf16[128,4,14337]{2,1,0:T(4,128)(2,1)}, u32[]{:S(2)}, u32[]{:S(2)}) async-start(bf16[128,4,14337]{2,1,0:T(4,128)(2,1)} %pad_maximum_fusion), calls=%async_computation | async-start | bytes 29622272 | tf_op jit(solution)/shard_map/all_to_all | solution.py:27
  47.7 211.5 %all-gather.3.cloned.1.call-start = ((), (), s32[]{:S(2)}) async-start(), calls=%async_computation.5 | async-start | bytes 3899392 | tf_op jit(solution)/shard_map/all_gather | solution.py:87
  48.4 369.1 %reduce-scatter.4.cloned.1.call-start = ((), (), s32[]{:S(2)}) async-start(), calls=%async_computation.7 | async-start | bytes 6193152
  124.6 3.9 copy-start.3
  124.6 4.3 copy-start.6
  259.1 3.9 copy-start.4
  263.7 2.0 copy-start.8
  277.9 2.8 copy-start.7
  289.8 69.3 %all-to-all-start.2 = ((bf16[16,16,7168]{2,1,0:T(8,128)(2,1)}), bf16[16,16,7168]{2,1,0:T(8,128)(2,1)}, u32[]{:S(2)}, u32[]{:S(2)}) async-start(bf16[16,16,7168]{2,1,0:T(8,128)(2,1)} %bitcast.95), calls=%async_computation.2 | async-start | bytes 7340032 | tf_op jit(solution)/shard_map/all_to_all | solution.py:19
  339.0 5.8 %copy-start.1 = (bf16[512,7168]{1,0:T(8,128)(2,1)S(1)}, bf16[512,7168]{1,0:T(8,128)(2,1)}, u32[]{:S(2)}) copy-start(bf16[512,7168]{1,0:T(8,128)(2,1)} %reshape.93) | copy-start | bytes 22020100
  339.0 5.8 %copy-start.5 = (bf16[1,7168,128]{2,1,0:T(8,128)(2,1)S(1)}, bf16[1,7168,128]{2,1,0:T(8,128)(2,1)}, u32[]{:S(2)}) copy-start(bf16[1,7168,128]{2,1,0:T(8,128)(2,1)} %param.15) | copy-start | bytes 5505028
  344.8 3.1 copy-start.2
  344.8 3.6 copy-start.9
  359.1 30.9 %all-to-all-start.3 = ((bf16[128,1,4]{2,1,0:T(2,128)(2,1)}), bf16[128,1,4]{2,1,0:T(2,128)(2,1)S(1)}, u32[]{:S(2)}, u32[]{:S(2)}) async-start(bf16[128,1,4]{2,1,0:T(2,128)(2,1)} %convert_element_type.134), calls=%async_computation.3 | async-start | bytes 131072 | tf_op jit(solution)/shard_map/all_to_all | solution.py:172
  390.0 99.5 %all-to-all-start.1 = ((bf16[128,4,7168]{2,1,0:T(4,128)(2,1)}), bf16[128,4,7168]{2,1,0:T(4,128)(2,1)}, u32[]{:S(2)}, u32[]{:S(2)}) async-start(bf16[128,4,7168]{2,1,0:T(4,128)(2,1)} %reshape.94), calls=%async_computation.1 | async-start | bytes 14680064 | tf_op jit(solution)/shard_map/all_to_all | solution.py:165
  400.4 9.4 %slice-start = ((s8[7340032]{0:T(1024)(128)(4,1)}), s8[4194304]{0:T(1024)(128)(4,1)S(1)}, s32[]{:S(2)}) async-start(s8[7340032]{0:T(1024)(128)(4,1)} %bitcast.89), calls=%async_computation.8 | async-start | bytes 8388608
  403.2 6.6 %slice-start.1 = ((s8[7340032]{0:T(1024)(128)(4,1)}), s8[3145728]{0:T(1024)(128)(4,1)S(1)}, s32[]{:S(2)}) async-start(s8[7340032]{0:T(1024)(128)(4,1)} %bitcast.89), calls=%async_computation.9 | async-start | bytes 6291456
  403.2 10.0 %slice-start.2 = ((s8[7340032]{0:T(1024)(128)(4,1)}), s8[4194304]{0:T(1024)(128)(4,1)S(1)}, s32[]{:S(2)}) async-start(s8[7340032]{0:T(1024)(128)(4,1)} %bitcast.91), calls=%async_computation.10 | async-start | bytes 8388608
  409.8 3.4 slice-start.3
  413.2 3.6 copy-start.10
Sparse Core Ops, SparseCore 0:
  10.1 114.4 all-gather.4
  126.7 132.3 all-gather.2
  278.0 42.8 reduce-scatter.3
where the time goes:
time: 516 us; the launch traced here: 506 us
  waiting for transfers between devices  283 us (55%)
  local copies, waits for them, and re-layouts  78.6 us (15%)
  matrix products  64.5 us (12%)
  starting transfers between devices  38 us (7%)
  other arithmetic  27.8 us (5%)
  between operations  14.5 us (3%)
    all_gather x1, waiting for transfers between devices, shared_part(): lax.all_gather(grad_out, 'local', axis=0, tiled=True)  129 us
    all_gather x1, waiting for transfers between devices, shared_part(): lax.all_gather(tokens, 'local', axis=0, tiled=True)  75.9 us
    all_to_all x1, waiting for transfers between devices, routed_part(): lax.all_to_all(partial_value.reshape(got_in.shape), ('node', 'local'), sp...  69.9 us
    dot_general x4, matrix products, contract_last(): lax.dot_general(left, right, (((1,), (1,)), ((), ())), preferred_element_...  23.7 us
    dot_general x6, matrix products, contract_first(): lax.dot_general(left, right, (((0,), (0,)), ((), ())), preferred_element_...  15.5 us
    slice x1, local copies, waits for them, and re-layouts, in_one_piece(): piece = out[..., at:at + column.shape[along]]  15.2 us
    reshape x1, local copies, waits for them, and re-layouts, routed_part(): partial_value.reshape(got_in.shape)  12.7 us
    reshape x1, local copies, waits for them, and re-layouts, routed_part(): got_grad.reshape(-1, width)  12.1 us
  transfers between devices with their start and end apart: 7, of which 4 were waited for; matrix products, arithmetic and copies ran while one was open for 31% of the time, Pallas kernels for 0%

commit v1 on v0

v1 whole, which is shorter than its diff:
```python
import jax
import jax.numpy as jnp
from jax import lax
from jax.experimental import pallas as pl
from jax.experimental.pallas import tpu as pltpu
from jax.sharding import PartitionSpec as P

MESH = pl.DeviceIdType.MESH
F32 = jnp.float32
BF16 = jnp.bfloat16
UNIT = 128
ROWS = 16
RING = 4


def dot(a, b, ca, cb):
    return lax.dot_general(a, b, (((ca,), (cb,)), ((), ())), preferred_element_type=F32)


def body(
    h_ref, wg_ref, wu_ref, wd_ref, sg_ref, su_ref, sd_ref,
    ret_ref, dwg_ref, dwu_ref, dwd_ref, dsg_ref, dsu_ref, dsd_ref,
    tt, tg, xx, w_all, v_all, gg, acc_p, acc_u,
    r1, r2, q1, q2, sw, pw, z1, z2, dw, out, ds,
    send_sem, recv_sem, load_sem, store_sem,
):
    width = wg_ref.shape[1]
    wide = width + UNIT
    block = width // 8
    half_block = block // 2
    node, here = lax.axis_index("node"), lax.axis_index("local")
    z, core = node // 2, node % 2
    y, x = here // RING, here % RING

    def step(v, by):
        return (v + by) % RING

    x_plus, x_minus = (node, y * RING + step(x, 1)), (node, y * RING + step(x, 3))
    y_plus, y_minus = (node, step(y, 1) * RING + x), (node, step(y, 3) * RING + x)
    z_plus, z_minus = (step(z, 1) * 2 + core, here), (step(z, 3) * 2 + core, here)
    partner = (z * 2 + (1 - core), here)
    first = ((x_plus, x_minus), (y_plus, y_minus))
    second = ((y_plus, y_minus), (x_plus, x_minus))

    loads = []

    def load(src, dst):
        copy = pltpu.make_async_copy(src, dst, load_sem.at[len(loads)])
        copy.start()
        loads.append(copy)

    for h in range(2):
        load(h_ref.at[h, :, pl.ds(0, wide)], tt.at[h, 0, 0])
        load(h_ref.at[h, :, pl.ds(wide, width)], tg.at[h, 0, 0])
    for i, ref in enumerate((wg_ref.at[0], wu_ref.at[0], sg_ref, su_ref)):
        load(ref, w_all.at[:, pl.ds(i * UNIT, UNIT)])
    for i, ref in enumerate((wd_ref.at[0], sd_ref)):
        load(ref, v_all.at[:, pl.ds(i * UNIT, UNIT)])

    barrier = pltpu.get_barrier_semaphore()
    for device in (x_plus, x_minus, y_plus, y_minus, z_plus, z_minus, partner):
        pl.semaphore_signal(barrier, inc=1, device_id=device, device_id_type=MESH)
    pl.semaphore_wait(barrier, 7)

    sends = []

    def send(src, dst, device):
        copy = pltpu.make_async_remote_copy(
            src_ref=src, dst_ref=dst, send_sem=send_sem.at[len(sends)],
            recv_sem=recv_sem.at[len(sends)], device_id=device, device_id_type=MESH,
        )
        copy.start()
        sends.append(copy)
        return copy

    for copy in loads[:4]:
        copy.wait()
    one = {}
    for part in range(2):
        for h in range(2):
            plus, minus = first[h]
            a, b = (tt, tg) if part == 0 else (tg, tt)
            one[h, "p", part] = send(a.at[h, 0, 0], a.at[h, 0, 3], plus)
            one[h, "m", part] = send(b.at[h, 0, 0], b.at[h, 0, 1], minus)
    far = {}
    for h in range(2):
        plus, minus = first[h]
        one[h, "p", 0].wait_recv()
        far[h, "p"] = send(tt.at[h, 0, 3], tt.at[h, 0, 2], plus)
        one[h, "m", 0].wait_recv()
        far[h, "m"] = send(tg.at[h, 0, 1], tg.at[h, 0, 2], minus)
    two = {}

    def second_hop(h, d):
        plus, minus = second[h]
        two[h, d, "pt"] = send(tt.at[h, 0, d], tt.at[h, 3, d], plus)
        two[h, d, "mg"] = send(tg.at[h, 0, d], tg.at[h, 1, d], minus)
        two[h, d, "pg"] = send(tg.at[h, 0, d], tg.at[h, 3, d], plus)
        two[h, d, "mt"] = send(tt.at[h, 0, d], tt.at[h, 1, d], minus)

    for h in range(2):
        second_hop(h, 0)
    for h in range(2):
        one[h, "p", 1].wait_recv()
        second_hop(h, 3)
    for h in range(2):
        one[h, "m", 1].wait_recv()
        second_hop(h, 1)
    for h in range(2):
        far[h, "p"].wait_recv()
        far[h, "m"].wait_recv()
        second_hop(h, 2)

    rows = 2 * RING * ROWS
    expert = here // (RING * RING // 2)
    lane = lax.broadcasted_iota(jnp.int32, (RING * ROWS, UNIT), 1)
    depth = width // 7

    def compute(i):
        acc_p[...] = jnp.zeros_like(acc_p)
        acc_u[...] = jnp.zeros_like(acc_u)

        def forward(k, carry):
            at = pl.ds(pl.multiple_of(k * depth, UNIT), depth)
            t = jnp.concatenate([tt[h, i, :, :, at].reshape(rows // 2, depth) for h in range(2)], 0)
            g = jnp.concatenate([tg[h, i, :, :, at].reshape(rows // 2, depth) for h in range(2)], 0)
            acc_p[...] += dot(t, w_all[at, :], 1, 0)
            acc_u[...] += dot(g, v_all[at, :], 1, 0)
            return carry

        lax.fori_loop(0, 7, forward, 0)
        for h in range(2):
            mine = slice(h * rows // 2, (h + 1) * rows // 2)
            side = tt[h, i, :, :, width:].reshape(rows // 2, UNIT).astype(F32)
            gate = jnp.where(expert == 0, side[:, 0:1], side[:, 1:2])
            for j, weight in enumerate((gate, side[:, 2:3])):
                pre = acc_p[mine, 2 * j * UNIT : (2 * j + 1) * UNIT]
                up = acc_p[mine, (2 * j + 1) * UNIT : (2 * j + 2) * UNIT]
                upstream = acc_u[mine, j * UNIT : (j + 1) * UNIT]
                sig = 1.0 / (1.0 + jnp.exp(-pre))
                activ = pre * sig
                slope = sig * (1.0 + pre * (1.0 - sig))
                hidden = activ * up
                scaled = weight * upstream
                for place, value in (
                    (2 * j, scaled * up * slope),
                    (2 * j + 1, scaled * activ),
                    (4 + j, weight * hidden),
                ):
                    gg[h, i, :, :, place * UNIT : (place + 1) * UNIT] = value.astype(BF16).reshape(
                        RING, ROWS, UNIT
                    )
                if j == 0:
                    score = jnp.sum(hidden * upstream, axis=1, keepdims=True)
                    xx[h, i, :, :, width:] = (
                        jnp.where(lane == expert, score, 0.0).astype(BF16).reshape(RING, ROWS, UNIT)
                    )

        def backward(k, carry):
            at = pl.ds(pl.multiple_of(k * (depth // 2), UNIT), depth // 2)
            g = jnp.concatenate(
                [gg[h, i, :, :, : 4 * UNIT].reshape(rows // 2, 4 * UNIT) for h in range(2)], 0
            )
            value = dot(g, w_all[at, :], 1, 1).astype(BF16)
            for h in range(2):
                xx[h, i, :, :, at] = value[h * rows // 2 : (h + 1) * rows // 2].reshape(
                    RING, ROWS, depth // 2
                )
            return carry

        lax.fori_loop(0, 14, backward, 0)

    for copy in loads[4:]:
        copy.wait()
    compute(0)
    onward = {}
    for d in (0, 3, 1, 2):
        for h in range(2):
            plus, minus = second[h]
            two[h, d, "pt"].wait_recv()
            onward[h, d, "p"] = send(tt.at[h, 3, d], tt.at[h, 2, d], plus)
            two[h, d, "mg"].wait_recv()
            onward[h, d, "m"] = send(tg.at[h, 1, d], tg.at[h, 2, d], minus)
    for d in range(RING):
        for h in range(2):
            two[h, d, "pg"].wait_recv()
            two[h, d, "mt"].wait_recv()
    compute(1)
    compute(3)
    for copy in onward.values():
        copy.wait_recv()
    compute(2)

    upper, lower = (2, 1), (3, 0)
    back = {}
    for h in range(2):
        plus, minus = second[h]
        for j in range(2):
            back[h, "p", j] = send(xx.at[h, 2, upper[j]], r1.at[h, 0, j], plus)
            back[h, "m", j] = send(xx.at[h, 2, lower[j]], r1.at[h, 1, j], minus)
    full = {}
    for h in range(2):
        plus, minus = second[h]
        for j in range(2):
            full[h, "p", lower[j]] = send(xx.at[h, 1, lower[j]], r2.at[h, 0, lower[j]], plus)
            full[h, "m", upper[j]] = send(xx.at[h, 3, upper[j]], r2.at[h, 1, upper[j]], minus)

    stores = []

    def store(src, dst):
        copy = pltpu.make_async_copy(src, dst, store_sem.at[len(stores)])
        copy.start()
        stores.append(copy)

    everything = 2 * RING * RING * ROWS

    def weights(parity):
        def one_block(k, carry):
            b = 2 * k + parity
            at = pl.ds(pl.multiple_of(b * block, UNIT), block)
            t = tt[:, :, :, :, at].reshape(everything, block)
            g = tg[:, :, :, :, at].reshape(everything, block)
            a = dot(t, gg[:, :, :, :, : 4 * UNIT].reshape(everything, 4 * UNIT), 0, 0)
            c = dot(g, gg[:, :, :, :, 4 * UNIT :].reshape(everything, 2 * UNIT), 0, 0)
            dw[0, b] = a[:, :UNIT].astype(BF16)
            dw[1, b] = a[:, UNIT : 2 * UNIT].astype(BF16)
            dw[2, b] = c[:, :UNIT].astype(BF16)
            sw[parity, k, :, : 2 * UNIT] = a[:, 2 * UNIT :].astype(BF16)
            sw[parity, k, :, 2 * UNIT :] = c[:, UNIT:].astype(BF16)
            return carry

        lax.fori_loop(0, RING, one_block, 0)

    def add(dst, *srcs):
        total = dst[...].astype(F32)
        for src in srcs:
            total = total + src[...].astype(F32)
        dst[...] = total.astype(BF16)

    weights(1 - core)
    swap = send(sw.at[1 - core], pw, partner)
    for j in range(2):
        for h in range(2):
            plus, minus = second[h]
            back[h, "p", j].wait_recv()
            add(xx.at[h, 1, upper[j]], r1.at[h, 0, j])
            full[h, "p", upper[j]] = send(xx.at[h, 1, upper[j]], r2.at[h, 0, upper[j]], plus)
            back[h, "m", j].wait_recv()
            add(xx.at[h, 3, lower[j]], r1.at[h, 1, j])
            full[h, "m", lower[j]] = send(xx.at[h, 3, lower[j]], r2.at[h, 1, lower[j]], minus)
    weights(core)
    for b in range(8):
        for j, ref in enumerate((dwg_ref, dwu_ref, dwd_ref)):
            store(dw.at[j, b], ref.at[0, pl.ds(b * block, block)])
    swap.wait_recv()

    def add_swap(k, carry):
        add(sw.at[core, k], pw.at[k])
        return carry

    lax.fori_loop(0, RING, add_swap, 0)
    low, high = pl.ds(0, half_block), pl.ds(half_block, half_block)
    z_back = (
        send(sw.at[core, step(z, 2), low], z1.at[0], z_plus),
        send(sw.at[core, step(z, 2), high], z1.at[1], z_minus),
    )
    z_full = [
        send(sw.at[core, step(z, 1), high], z2.at[0, high], z_plus),
        send(sw.at[core, step(z, 3), low], z2.at[1, low], z_minus),
    ]

    cut = (wide // UNIT + 1) // 2 * UNIT
    left, right = pl.ds(0, cut), pl.ds(cut, wide - cut)
    for d in (2, 3, 1, 0):
        for h in range(2):
            full[h, "p", d].wait_recv()
            full[h, "m", d].wait_recv()
            add(xx.at[h, 0, d], r2.at[h, 0, d], r2.at[h, 1, d])
            plus, minus = first[h]
            if d == 2:
                back[h, "P"] = send(xx.at[h, 0, 2, :, left], q1.at[h, 0, :, left], plus)
                back[h, "M"] = send(xx.at[h, 0, 2, :, right], q1.at[h, 1, :, right], minus)
            if d == 1:
                full[h, "P"] = send(xx.at[h, 0, 1, :, right], q2.at[h, 0, :, right], plus)
            if d == 3:
                full[h, "M"] = send(xx.at[h, 0, 3, :, left], q2.at[h, 1, :, left], minus)
    z_back[0].wait_recv()
    add(sw.at[core, step(z, 1), low], z1.at[0])
    z_full.append(send(sw.at[core, step(z, 1), low], z2.at[0, low], z_plus))
    z_back[1].wait_recv()
    add(sw.at[core, step(z, 3), high], z1.at[1])
    z_full.append(send(sw.at[core, step(z, 3), high], z2.at[1, high], z_minus))
    last = []
    for h in range(2):
        plus, minus = first[h]
        back[h, "P"].wait_recv()
        add(xx.at[h, 0, 1, :, left], q1.at[h, 0, :, left])
        last.append(send(xx.at[h, 0, 1, :, left], q2.at[h, 0, :, left], plus))
        back[h, "M"].wait_recv()
        add(xx.at[h, 0, 3, :, right], q1.at[h, 1, :, right])
        last.append(send(xx.at[h, 0, 3, :, right], q2.at[h, 1, :, right], minus))
    for copy in last:
        copy.wait_recv()
    for h in range(2):
        full[h, "P"].wait_recv()
        full[h, "M"].wait_recv()
        total = xx[h, 0, 0].astype(F32) + q2[h, 0].astype(F32) + q2[h, 1].astype(F32)
        out[h] = total.astype(BF16)
    store(out, ret_ref)
    for copy in z_full:
        copy.wait_recv()
    total = sw[core, z].astype(F32) + z2[0].astype(F32) + z2[1].astype(F32)
    for j, ref in enumerate((dsg_ref, dsu_ref, dsd_ref)):
        ds[j] = total[:, j * UNIT : (j + 1) * UNIT].astype(BF16)
        store(ds.at[j], ref)
    for copy in sends:
        copy.wait_send()
    for copy in stores:
        copy.wait()


SENDS = 8 + 4 + 32 + 16 + 8 + 8 + 8 + 1 + 6 + 4 * 2 + 4


def expert_layer(rows, w_gate, w_up, w_down, s_gate, s_up, s_down):
    width = s_gate.shape[0]
    wide = width + UNIT
    block = width // 8
    shape = jax.ShapeDtypeStruct
    return pl.pallas_call(
        body,
        out_shape=(
            shape((2, ROWS, wide), BF16),
            *(shape(w_gate.shape, BF16) for _ in range(3)),
            *(shape((block, UNIT), BF16) for _ in range(3)),
        ),
        in_specs=[pl.BlockSpec(memory_space=pl.ANY)] * 7,
        out_specs=(pl.BlockSpec(memory_space=pl.ANY),) * 7,
        scratch_shapes=[
            pltpu.VMEM((2, RING, RING, ROWS, wide), BF16),
            pltpu.VMEM((2, RING, RING, ROWS, width), BF16),
            pltpu.VMEM((2, RING, RING, ROWS, wide), BF16),
            pltpu.VMEM((width, 4 * UNIT), BF16),
            pltpu.VMEM((width, 2 * UNIT), BF16),
            pltpu.VMEM((2, RING, RING, ROWS, 6 * UNIT), BF16),
            pltpu.VMEM((2 * RING * ROWS, 4 * UNIT), F32),
            pltpu.VMEM((2 * RING * ROWS, 2 * UNIT), F32),
            pltpu.VMEM((2, 2, 2, ROWS, wide), BF16),
            pltpu.VMEM((2, 2, RING, ROWS, wide), BF16),
            pltpu.VMEM((2, 2, ROWS, wide), BF16),
            pltpu.VMEM((2, 2, ROWS, wide), BF16),
            pltpu.VMEM((2, RING, block, 3 * UNIT), BF16),
            pltpu.VMEM((RING, block, 3 * UNIT), BF16),
            pltpu.VMEM((2, block // 2, 3 * UNIT), BF16),
            pltpu.VMEM((2, block, 3 * UNIT), BF16),
            pltpu.VMEM((3, 8, block, UNIT), BF16),
            pltpu.VMEM((2, ROWS, wide), BF16),
            pltpu.VMEM((3, block, UNIT), BF16),
            pltpu.SemaphoreType.DMA((SENDS,)),
            pltpu.SemaphoreType.DMA((SENDS,)),
            pltpu.SemaphoreType.DMA((10,)),
            pltpu.SemaphoreType.DMA((28,)),
        ],
        compiler_params=pltpu.CompilerParams(
            collective_id=0, has_side_effects=True, vmem_limit_bytes=67043328
        ),
    )(rows, w_gate, w_up, w_down, s_gate, s_up, s_down)


def local(tokens, grad_out, gates, expert_ids, w_gate, w_up, w_down, s_gate, s_up, s_down):
    count, width = tokens.shape
    nodes = lax.axis_size("node")
    slots = 2 * count // nodes
    places = jnp.arange(slots, dtype=jnp.int32)
    pair = 2 * jnp.arange(nodes, dtype=jnp.int32)[None, :]
    chosen = [expert_ids[:, :, None] == (pair + e)[:, None, :] for e in range(2)]
    gate = gates.astype(F32)[:, :, None]
    weight = [jnp.sum(jnp.where(c, gate, 0.0), axis=1) for c in chosen]
    named = [jnp.any(c, axis=1) for c in chosen]
    member = named[0] | named[1]
    both = (named[0] & named[1]).astype(F32)
    ranking = jnp.cumsum(member.astype(jnp.int32), axis=0) - 1
    pick = (member[:, :, None] & (ranking[:, :, None] == places)).astype(BF16)
    side = jnp.stack([weight[0], weight[1], both], axis=-1)
    side = jnp.sum(pick.astype(F32)[..., None] * side[:, :, None, :], axis=0)
    side = jnp.pad(side, ((0, 0), (0, 0), (0, UNIT - 3))).astype(BF16)
    pieces = [
        jnp.einsum("tns,td->nsd", pick, value, preferred_element_type=F32).astype(BF16)
        for value in (tokens, grad_out)
    ]
    rows = jnp.concatenate([pieces[0], side, pieces[1]], axis=2)
    rows = lax.all_to_all(rows, "node", split_axis=0, concat_axis=0, tiled=True)
    rows = rows.reshape(2, ROWS, rows.shape[2])
    ret, dwg, dwu, dwd, dsg, dsu, dsd = expert_layer(
        rows, w_gate, w_up, w_down, s_gate, s_up, s_down
    )
    ret = ret.reshape(nodes, slots, ret.shape[2])
    ret = lax.all_to_all(ret, "node", split_axis=0, concat_axis=0, tiled=True)
    dx = jnp.einsum("tns,nsd->td", pick, ret[:, :, :width], preferred_element_type=F32)
    score = ret[:, :, width : width + 2].astype(F32)
    score = jnp.sum(pick.astype(F32)[..., None] * score[None], axis=2)
    dgates = sum(
        jnp.sum(jnp.where(chosen[e], score[:, None, :, e], 0.0), axis=2) for e in range(2)
    )
    return dx.astype(BF16), dgates, dwg, dwu, dwd, dsg, dsu, dsd


def solution(mesh):
    flat = P(("node", "local"), None)
    routed = P("node", None, "local")
    shared = P(None, "local")
    return jax.shard_map(
        local,
        mesh=mesh,
        in_specs=(flat,) * 4 + (routed,) * 3 + (shared,) * 3,
        out_specs=(flat, flat) + (routed,) * 3 + (P("node", "local"),) * 3,
        check_vma=False,
    )
```

time: 516 us -> 185 us (0.36)
  the two profiles are of different devices: /device:TPU:11 before, /device:TPU:0 now
where the time goes in v1:
time: 185 us; the launch traced here: 184 us
  Pallas kernels  131 us (71%)
  blocking collectives  19.9 us (11%)
  local copies, waits for them, and re-layouts  12.4 us (7%)
  waiting for transfers between devices  9.63 us (5%)
  starting transfers between devices  3.48 us (2%)
  matrix products  3.34 us (2%)
  other arithmetic  3.17 us (2%)
    pallas_call x1, Pallas kernels, expert_layer(): pl.pallas_call(body, out_shape=(shape((2, ROWS, wide), BF16), *(shape(w_g...  131 us
    all_to_all x1, blocking collectives, local(): rows = lax.all_to_all(rows, 'node', split_axis=0, concat_axis=0, tiled=True)  19.9 us
    all_to_all x1, waiting for transfers between devices, local(): ret = lax.all_to_all(ret, 'node', split_axis=0, concat_axis=0, tiled=True)  9.63 us
    unnamed x42, local copies, waits for them, and re-layouts  8.51 us
  transfers between devices with their start and end apart: 1, of which 1 were waited for; matrix products, arithmetic and copies ran while one was open for 0% of the time, Pallas kernels for 0%

profile of v1, /device:TPU:0, one launch (start us, length us, event | category | flops | bytes accessed | tf_op | source)
XLA Modules:
  0.0 184.2 jit_solution(11171601298952372485)
XLA Ops:
  0.7 0.7 convert_element_type.57
  1.4 0.8 compare_reduce_fusion
  2.1 0.8 fusion.13
  3.1 0.6 copy-done.6
  3.9 1.2 convolution_convert_fusion
  5.1 1.2 convolution_convert_fusion.1
  6.4 0.4 copy.51
  6.8 19.9 %all_to_all.10 = bf16[8,4,14464]{2,1,0:T(4,128)(2,1)S(1)} all-to-all(bf16[8,4,14464]{2,1,0:T(4,128)(2,1)S(1)} %copy.51), channel_id=1, replica_groups=mesh['node'=8,'local'=16] {'node'}, dimensions={0} | all-to-all | bytes 1851392 | tf_op jit(solution)/shard_map/all_to_all | solution.py:392
  26.7 1.1 reshape.78.h_ref
  27.8 131.5 %shard_map.161 = (bf16[2,16,7296]{2,1,0:T(8,128)(2,1)}, bf16[1,7168,128]{2,1,0:T(8,128)(2,1)}, bf16[1,7168,128]{2,1,0:T(8,128)(2,1)}, bf16[1,7168,128]{2,1,0:T(8...) custom-call(bf16[2,16,14464]{2,1,0:T(8,128)(2,1)} %reshape.78.h_ref, ...), custom_call_target="tpu_custom_call" | custom-call | tf_op jit(solution)/shard_map/pallas_call | solution.py:330
  159.4 2.0 %reshape.79 = bf16[8,4,7296]{2,1,0:T(4,128)(2,1)} reshape(bf16[2,16,7296]{2,1,0:T(8,128)(2,1)} %get-tuple-element.15) | data formatting | bytes 933888 | tf_op jit(solution)/shard_map/reshape | solution.py:397
  161.4 3.5 %all-to-all-start.1 = ((bf16[8,4,7296]{2,1,0:T(4,128)(2,1)}), bf16[8,4,7296]{2,1,0:T(4,128)(2,1)S(1)}, u32[]{:S(2)}, u32[]{:S(2)}) async-start(bf16[8,4,7296]{2,1,0:T(4,128)(2,1)} %reshape.79), calls=%async_computation.1 | async-start | bytes 933888 | tf_op jit(solution)/shard_map/all_to_all | solution.py:398
  164.9 9.6 %all-to-all-done.1 = bf16[8,4,7296]{2,1,0:T(4,128)(2,1)S(1)} async-done(((bf16[8,4,7296]{2,1,0:T(4,128)(2,1)}), bf16[8,4,7296]{2,1,0:T(4,128)(2,1)S(1)}, u32[]{:S(2)}, u32[]{:S(2)}) %all-to-all-start.1) | async-done | bytes 466976 | tf_op jit(solution)/shard_map/all_to_all | solution.py:398
  174.5 0.2 slice.16
  174.7 1.0 fusion
  176.0 0.6 add.20
  176.6 1.2 copy.68
  177.8 0.9 copy-done.1
  178.7 1.2 copy.69
  180.0 0.9 copy-done
  180.9 1.2 copy.70
  182.1 0.7 copy.71
  182.8 0.7 copy.72
  183.5 0.7 copy.73
  (49 shorter events, 0.9 us)
Async XLA Ops:
  0.6 2.2 %copy-start.13 = (s32[8]{0:T(128)}, s32[8]{0:T(128)S(1)}, u32[]{:S(2)}) copy-start(s32[8]{0:T(128)S(1)} %get-tuple-element.33) | copy-start | bytes 100
  0.7 2.2 %copy-start.15 = (s32[8]{0:T(128)}, s32[8]{0:T(128)S(1)}, u32[]{:S(2)}) copy-start(s32[8]{0:T(128)S(1)} %get-tuple-element.34) | copy-start | bytes 100
  2.9 3.5 %copy-start.10 = (pred[16,8]{0,1:T(8,128)(4,1)}, pred[16,8]{0,1:T(8,128)(4,1)S(1)}, u32[]{:S(2)}) copy-start(pred[16,8]{0,1:T(8,128)(4,1)S(1)} %get-tuple-element.29) | copy-start | bytes 388
  3.1 3.3 %copy-start.8 = (s32[16,8]{0,1:T(8,128)}, s32[16,8]{0,1:T(8,128)S(1)}, u32[]{:S(2)}) copy-start(s32[16,8]{0,1:T(8,128)S(1)} %copy.48) | copy-start | bytes 1540
  3.1 0.6 copy-start.6
  159.3 15.4 %copy-start.9 = (s32[16,8]{0,1:T(8,128)S(1)}, s32[16,8]{0,1:T(8,128)}, u32[]{:S(2)}) copy-start(s32[16,8]{0,1:T(8,128)} %copy-done.8) | copy-start | bytes 1540
  159.3 15.4 %copy-start.11 = (pred[16,8]{0,1:T(8,128)(4,1)S(1)}, pred[16,8]{0,1:T(8,128)(4,1)}, u32[]{:S(2)}) copy-start(pred[16,8]{0,1:T(8,128)(4,1)} %copy-done.10) | copy-start | bytes 388
  159.3 16.5 %copy-start.7 = (f32[16,8,4]{0,1,2:T(8,128)S(1)}, f32[16,8,4]{0,1,2:T(8,128)}, u32[]{:S(2)}) copy-start(f32[16,8,4]{0,1,2:T(8,128)} %copy-done.6) | copy-start | bytes 6148
  159.3 16.6 %copy-start.12 = (s32[16,3]{0,1:T(4,128)S(1)}, s32[16,3]{0,1:T(4,128)}, u32[]{:S(2)}) copy-start(s32[16,3]{0,1:T(4,128)} %param.13) | copy-start | bytes 580
  159.3 16.5 %copy-start.14 = (s32[8]{0:T(128)S(1)}, s32[8]{0:T(128)}, u32[]{:S(2)}) copy-start(s32[8]{0:T(128)} %copy-done.13) | copy-start | bytes 100
  159.3 16.5 %copy-start.16 = (s32[8]{0:T(128)S(1)}, s32[8]{0:T(128)}, u32[]{:S(2)}) copy-start(s32[8]{0:T(128)} %copy-done.15) | copy-start | bytes 100
  159.4 17.2 %copy-start.2 = (bf16[1,7168,128]{2,1,0:T(8,128)(2,1)S(1)}, bf16[1,7168,128]{2,1,0:T(8,128)(2,1)}, u32[]{:S(2)}) copy-start(bf16[1,7168,128]{2,1,0:T(8,128)(2,1)} %get-tuple-element.45) | copy-start | bytes 5505028
  161.4 13.1 %all-to-all-start.1 = ((bf16[8,4,7296]{2,1,0:T(4,128)(2,1)}), bf16[8,4,7296]{2,1,0:T(4,128)(2,1)S(1)}, u32[]{:S(2)}, u32[]{:S(2)}) async-start(bf16[8,4,7296]{2,1,0:T(4,128)(2,1)} %reshape.79), calls=%async_computation.1 | async-start | bytes 933888 | tf_op jit(solution)/shard_map/all_to_all | solution.py:398
  176.6 2.2 %copy-start.1 = (bf16[1,7168,128]{2,1,0:T(8,128)(2,1)S(1)}, bf16[1,7168,128]{2,1,0:T(8,128)(2,1)}, u32[]{:S(2)}) copy-start(bf16[1,7168,128]{2,1,0:T(8,128)(2,1)} %get-tuple-element.46) | copy-start | bytes 5505028
  178.7 2.2 %copy-start = (bf16[1,7168,128]{2,1,0:T(8,128)(2,1)S(1)}, bf16[1,7168,128]{2,1,0:T(8,128)(2,1)}, u32[]{:S(2)}) copy-start(bf16[1,7168,128]{2,1,0:T(8,128)(2,1)} %get-tuple-element.47) | copy-start | bytes 5505028
  180.9 1.2 copy-start.5
  180.9 1.9 %copy-start.4 = (bf16[896,128]{1,0:T(8,128)(2,1)S(1)}, bf16[896,128]{1,0:T(8,128)(2,1)}, u32[]{:S(2)}) copy-start(bf16[896,128]{1,0:T(8,128)(2,1)} %get-tuple-element.49) | copy-start | bytes 688132
  180.9 2.6 %copy-start.3 = (bf16[896,128]{1,0:T(8,128)(2,1)S(1)}, bf16[896,128]{1,0:T(8,128)(2,1)}, u32[]{:S(2)}) copy-start(bf16[896,128]{1,0:T(8,128)(2,1)} %get-tuple-element.50) | copy-start | bytes 688132

commit v2 on v1

--- a/solution.py
+++ b/solution.py
@@ -18,10 +18,10 @@
 
 
 def body(
-    h_ref, wg_ref, wu_ref, wd_ref, sg_ref, su_ref, sd_ref,
-    ret_ref, dwg_ref, dwu_ref, dwd_ref, dsg_ref, dsu_ref, dsd_ref,
-    tt, tg, xx, w_all, v_all, gg, acc_p, acc_u,
-    r1, r2, q1, q2, sw, pw, z1, z2, dw, out, ds,
+    tok_ref, grad_ref, gate_ref, id_ref, wg_ref, wu_ref, wd_ref, sg_ref, su_ref, sd_ref,
+    dx_ref, dgate_ref, dwg_ref, dwu_ref, dwd_ref, dsg_ref, dsu_ref, dsd_ref,
+    given, outgo, income, relay, answer, reply, relay_back, tt, tg, xx, w_all, v_all, gg, acc_p, acc_u,
+    r1, r2, q1, q2, sw, pw, z1, z2, dw, ds,
     send_sem, recv_sem, load_sem, store_sem,
 ):
     width = wg_ref.shape[1]
@@ -39,6 +39,8 @@
     y_plus, y_minus = (node, step(y, 1) * RING + x), (node, step(y, 3) * RING + x)
     z_plus, z_minus = (step(z, 1) * 2 + core, here), (step(z, 3) * 2 + core, here)
     partner = (z * 2 + (1 - core), here)
+    z_plus_other = (step(z, 1) * 2 + (1 - core), here)
+    z_minus_other = (step(z, 3) * 2 + (1 - core), here)
     first = ((x_plus, x_minus), (y_plus, y_minus))
     second = ((y_plus, y_minus), (x_plus, x_minus))
 
@@ -49,18 +51,74 @@
         copy.start()
         loads.append(copy)
 
-    for h in range(2):
-        load(h_ref.at[h, :, pl.ds(0, wide)], tt.at[h, 0, 0])
-        load(h_ref.at[h, :, pl.ds(wide, width)], tg.at[h, 0, 0])
+    load(tok_ref, given.at[0])
+    load(grad_ref, given.at[1])
     for i, ref in enumerate((wg_ref.at[0], wu_ref.at[0], sg_ref, su_ref)):
         load(ref, w_all.at[:, pl.ds(i * UNIT, UNIT)])
     for i, ref in enumerate((wd_ref.at[0], sd_ref)):
         load(ref, v_all.at[:, pl.ds(i * UNIT, UNIT)])
 
     barrier = pltpu.get_barrier_semaphore()
-    for device in (x_plus, x_minus, y_plus, y_minus, z_plus, z_minus, partner):
+    for device in (
+        x_plus, x_minus, y_plus, y_minus, z_plus, z_minus, z_plus_other, z_minus_other, partner
+    ):
         pl.semaphore_signal(barrier, inc=1, device_id=device, device_id_type=MESH)
-    pl.semaphore_wait(barrier, 7)
+
+    count = ROWS
+    eye = lax.broadcasted_iota(jnp.int32, (count, count), 0) == lax.broadcasted_iota(
+        jnp.int32, (count, count), 1
+    )
+
+    def as_row(column):
+        return jnp.sum(jnp.where(eye, column, 0.0), axis=0, keepdims=True)
+
+    def as_column(row):
+        return jnp.sum(jnp.where(eye, row, 0.0), axis=1, keepdims=True)
+
+    slot_row = lax.broadcasted_iota(jnp.int32, (2 * ROWS, count), 0)
+    slot_node = ((z + (slot_row >> 3)) & 3) * 2 + ((core + (slot_row >> 2)) & 1)
+    ids = id_ref[...].astype(F32)
+    gates = gate_ref[...].astype(F32)
+    id_rows = [as_row(ids[:, k : k + 1]) for k in range(3)]
+    gate_rows = [as_row(gates[:, k : k + 1]) for k in range(3)]
+    names = [
+        [(id_rows[k] == (2 * slot_node + e).astype(F32)).astype(F32) for k in range(3)]
+        for e in range(2)
+    ]
+    named = [names[e][0] + names[e][1] + names[e][2] for e in range(2)]
+    member = jnp.maximum(named[0], named[1])
+    earlier = (
+        lax.broadcasted_iota(jnp.int32, (count, count), 0)
+        < lax.broadcasted_iota(jnp.int32, (count, count), 1)
+    ).astype(BF16)
+    ranking = dot(member.astype(BF16), earlier, 1, 0)
+    pick = jnp.where(ranking == (slot_row & 3).astype(F32), member, 0.0)
+    pick_bf16 = pick.astype(BF16)
+    side = [
+        jnp.sum(pick * sum(names[e][k] * gate_rows[k] for k in range(3)), axis=1, keepdims=True)
+        for e in range(2)
+    ]
+    side.append(jnp.sum(pick * named[0] * named[1], axis=1, keepdims=True))
+    slot_lane = lax.broadcasted_iota(jnp.int32, (2 * ROWS, UNIT), 1)
+    columns = sum(jnp.where(slot_lane == i, side[i], 0.0) for i in range(3)).astype(BF16)
+    for s in range(8):
+        outgo[s, :, width:wide] = columns[4 * s : 4 * s + 4]
+    for copy in loads[:2]:
+        copy.wait()
+    stretch = width // 7
+
+    def cut_rows(k, carry):
+        at = pl.multiple_of(k * stretch, UNIT)
+        for i, offset in enumerate((0, wide)):
+            value = dot(pick_bf16, given[i, :, pl.ds(at, stretch)], 1, 0)
+            for s in range(8):
+                outgo[s, :, pl.ds(pl.multiple_of(at + offset, UNIT), stretch)] = value[
+                    4 * s : 4 * s + 4
+                ].astype(BF16)
+        return carry
+
+    lax.fori_loop(0, 7, cut_rows, 0)
+    pl.semaphore_wait(barrier, 9)
 
     sends = []
 
@@ -73,23 +131,51 @@
         sends.append(copy)
         return copy
 
-    for copy in loads[:4]:
-        copy.wait()
-    one = {}
-    for part in range(2):
-        for h in range(2):
-            plus, minus = first[h]
-            a, b = (tt, tg) if part == 0 else (tg, tt)
+    across = {
+        (0, 1): send(outgo.at[1], income.at[1], partner),
+        (3, 0): send(outgo.at[6], income.at[2], z_minus),
+        (2, 0): send(outgo.at[4], relay.at[0], z_plus),
+        (3, 1): send(outgo.at[7], income.at[3], z_minus_other),
+        (1, 0): send(outgo.at[2], income.at[6], z_plus),
+        (2, 1): send(outgo.at[5], relay.at[1], z_minus),
+        (1, 1): send(outgo.at[3], income.at[7], z_plus_other),
+    }
+
+    def stack(h):
+        def piece(at, size):
+            return jnp.concatenate(
+                [
+                    (outgo if h == 0 and s == 0 else income)[4 * h + s, :, pl.ds(at, size)].astype(F32)
+                    for s in range(4)
+                ],
+                0,
+            ).astype(BF16)
+
+        def one_stretch(k, carry):
+            at = pl.multiple_of(k * stretch, UNIT)
+            tt[h, 0, 0, :, pl.ds(at, stretch)] = piece(at, stretch)
+            tg[h, 0, 0, :, pl.ds(at, stretch)] = piece(pl.multiple_of(at + wide, UNIT), stretch)
+            return carry
+
+        lax.fori_loop(0, 7, one_stretch, 0)
+        tt[h, 0, 0, :, width:] = piece(width, UNIT)
+
+    one, two, far = {}, {}, {}
+
+    def first_hop(h):
+        plus, minus = first[h]
+        for part, (a, b) in enumerate(((tt, tg), (tg, tt))):
             one[h, "p", part] = send(a.at[h, 0, 0], a.at[h, 0, 3], plus)
             one[h, "m", part] = send(b.at[h, 0, 0], b.at[h, 0, 1], minus)
-    far = {}
-    for h in range(2):
-        plus, minus = first[h]
-        one[h, "p", 0].wait_recv()
-        far[h, "p"] = send(tt.at[h, 0, 3], tt.at[h, 0, 2], plus)
-        one[h, "m", 0].wait_recv()
-        far[h, "m"] = send(tg.at[h, 0, 1], tg.at[h, 0, 2], minus)
-    two = {}
+
+    across[2, 0].wait_recv()
+    forth = [send(relay.at[0], income.at[4], z_plus)]
+    for key in ((0, 1), (3, 0), (3, 1)):
+        across[key].wait_recv()
+    stack(0)
+    first_hop(0)
+    across[2, 1].wait_recv()
+    forth.append(send(relay.at[1], income.at[5], z_minus_other))
 
     def second_hop(h, d):
         plus, minus = second[h]
@@ -98,8 +184,21 @@
         two[h, d, "pg"] = send(tg.at[h, 0, d], tg.at[h, 3, d], plus)
         two[h, d, "mt"] = send(tt.at[h, 0, d], tt.at[h, 1, d], minus)
 
-    for h in range(2):
-        second_hop(h, 0)
+    def pass_on(h):
+        plus, minus = first[h]
+        one[h, "p", 0].wait_recv()
+        far[h, "p"] = send(tt.at[h, 0, 3], tt.at[h, 0, 2], plus)
+        one[h, "m", 0].wait_recv()
+        far[h, "m"] = send(tg.at[h, 0, 1], tg.at[h, 0, 2], minus)
+
+    second_hop(0, 0)
+    for copy in (across[1, 0], across[1, 1], *forth):
+        copy.wait_recv()
+    stack(1)
+    first_hop(1)
+    pass_on(0)
+    second_hop(1, 0)
+    pass_on(1)
     for h in range(2):
         one[h, "p", 1].wait_recv()
         second_hop(h, 3)
@@ -170,7 +269,7 @@
 
         lax.fori_loop(0, 14, backward, 0)
 
-    for copy in loads[4:]:
+    for copy in loads[2:]:
         copy.wait()
     compute(0)
     onward = {}
@@ -187,23 +286,22 @@
             two[h, d, "mt"].wait_recv()
     compute(1)
     compute(3)
-    for copy in onward.values():
-        copy.wait_recv()
-    compute(2)
-
     upper, lower = (2, 1), (3, 0)
-    back = {}
-    for h in range(2):
-        plus, minus = second[h]
-        for j in range(2):
-            back[h, "p", j] = send(xx.at[h, 2, upper[j]], r1.at[h, 0, j], plus)
-            back[h, "m", j] = send(xx.at[h, 2, lower[j]], r1.at[h, 1, j], minus)
     full = {}
     for h in range(2):
         plus, minus = second[h]
         for j in range(2):
             full[h, "p", lower[j]] = send(xx.at[h, 1, lower[j]], r2.at[h, 0, lower[j]], plus)
             full[h, "m", upper[j]] = send(xx.at[h, 3, upper[j]], r2.at[h, 1, upper[j]], minus)
+    for copy in onward.values():
+        copy.wait_recv()
+    compute(2)
+    back = {}
+    for j in range(2):
+        for h in range(2):
+            plus, minus = second[h]
+            back[h, "p", j] = send(xx.at[h, 2, upper[j]], r1.at[h, 0, j], plus)
+            back[h, "m", j] = send(xx.at[h, 2, lower[j]], r1.at[h, 1, j], minus)
 
     stores = []
 
@@ -299,44 +397,102 @@
         back[h, "M"].wait_recv()
         add(xx.at[h, 0, 3, :, right], q1.at[h, 1, :, right])
         last.append(send(xx.at[h, 0, 3, :, right], q2.at[h, 1, :, right], minus))
-    for copy in last:
-        copy.wait_recv()
     for h in range(2):
         full[h, "P"].wait_recv()
         full[h, "M"].wait_recv()
-        total = xx[h, 0, 0].astype(F32) + q2[h, 0].astype(F32) + q2[h, 1].astype(F32)
-        out[h] = total.astype(BF16)
-    store(out, ret_ref)
+        last[2 * h].wait_recv()
+        last[2 * h + 1].wait_recv()
+
+        def one_stretch(k, carry, h=h):
+            at = pl.ds(pl.multiple_of(k * 3 * UNIT, UNIT), 3 * UNIT)
+            total = xx[h, 0, 0, :, at].astype(F32)
+            for i in range(2):
+                total = total + q2[h, i, :, at].astype(F32)
+            for s in range(4):
+                answer[4 * h + s, :, at] = total[4 * s : 4 * s + 4].astype(BF16)
+            return carry
+
+        lax.fori_loop(0, wide // (3 * UNIT), one_stretch, 0)
+        if h == 0:
+            home = [
+                send(answer.at[2], reply.at[6], z_plus),
+                send(answer.at[3], reply.at[7], z_plus_other),
+                send(answer.at[1], reply.at[1], partner),
+            ]
+        else:
+            home += [
+                send(answer.at[4], relay_back.at[0], z_plus),
+                send(answer.at[5], relay_back.at[1], z_minus),
+                send(answer.at[6], reply.at[2], z_minus),
+                send(answer.at[7], reply.at[3], z_minus_other),
+            ]
     for copy in z_full:
         copy.wait_recv()
     total = sw[core, z].astype(F32) + z2[0].astype(F32) + z2[1].astype(F32)
     for j, ref in enumerate((dsg_ref, dsu_ref, dsd_ref)):
         ds[j] = total[:, j * UNIT : (j + 1) * UNIT].astype(BF16)
         store(ds.at[j], ref)
+    home[3].wait_recv()
+    home.append(send(relay_back.at[0], reply.at[4], z_plus))
+    home[4].wait_recv()
+    home.append(send(relay_back.at[1], reply.at[5], z_minus_other))
+    for i in (0, 1, 2, 5, 6, 7, 8):
+        home[i].wait_recv()
+
+    def answers(at, size):
+        return jnp.concatenate(
+            [(answer if s == 0 else reply)[s, :, pl.ds(at, size)].astype(F32) for s in range(8)], 0
+        )
+
+    def finish(k, carry):
+        at = pl.multiple_of(k * stretch, UNIT)
+        total = dot(pick_bf16, answers(at, stretch).astype(BF16), 0, 0)
+        given[0, :, pl.ds(at, stretch)] = total.astype(BF16)
+        return carry
+
+    lax.fori_loop(0, 7, finish, 0)
+    store(given.at[0], dx_ref)
+    score = answers(width, UNIT)
+    for k in range(3):
+        row = jnp.sum(
+            pick * (names[0][k] * score[:, 0:1] + names[1][k] * score[:, 1:2]),
+            axis=0, keepdims=True,
+        )
+        dgate_ref[:, k : k + 1] = as_column(row)
     for copy in sends:
         copy.wait_send()
     for copy in stores:
         copy.wait()
 
 
-SENDS = 8 + 4 + 32 + 16 + 8 + 8 + 8 + 1 + 6 + 4 * 2 + 4
-
-
-def expert_layer(rows, w_gate, w_up, w_down, s_gate, s_up, s_down):
+SENDS = 103 + 9 + 9
+
+
+def expert_layer(tokens, grad_out, gates, ids, w_gate, w_up, w_down, s_gate, s_up, s_down):
     width = s_gate.shape[0]
     wide = width + UNIT
     block = width // 8
     shape = jax.ShapeDtypeStruct
+    anywhere = pl.BlockSpec(memory_space=pl.ANY)
+    inside = pl.BlockSpec(memory_space=pltpu.VMEM)
     return pl.pallas_call(
         body,
         out_shape=(
-            shape((2, ROWS, wide), BF16),
+            shape(tokens.shape, BF16),
+            shape(gates.shape, F32),
             *(shape(w_gate.shape, BF16) for _ in range(3)),
             *(shape((block, UNIT), BF16) for _ in range(3)),
         ),
-        in_specs=[pl.BlockSpec(memory_space=pl.ANY)] * 7,
-        out_specs=(pl.BlockSpec(memory_space=pl.ANY),) * 7,
+        in_specs=[anywhere] * 2 + [inside] * 2 + [anywhere] * 6,
+        out_specs=(anywhere, inside) + (anywhere,) * 6,
         scratch_shapes=[
+            pltpu.VMEM((2, ROWS, width), BF16),
+            pltpu.VMEM((8, 4, wide + width), BF16),
+            pltpu.VMEM((8, 4, wide + width), BF16),
+            pltpu.VMEM((2, 4, wide + width), BF16),
+            pltpu.VMEM((8, 4, wide), BF16),
+            pltpu.VMEM((8, 4, wide), BF16),
+            pltpu.VMEM((2, 4, wide), BF16),
             pltpu.VMEM((2, RING, RING, ROWS, wide), BF16),
             pltpu.VMEM((2, RING, RING, ROWS, width), BF16),
             pltpu.VMEM((2, RING, RING, ROWS, wide), BF16),
@@ -354,55 +510,16 @@
             pltpu.VMEM((2, block // 2, 3 * UNIT), BF16),
             pltpu.VMEM((2, block, 3 * UNIT), BF16),
             pltpu.VMEM((3, 8, block, UNIT), BF16),
-            pltpu.VMEM((2, ROWS, wide), BF16),
             pltpu.VMEM((3, block, UNIT), BF16),
             pltpu.SemaphoreType.DMA((SENDS,)),
             pltpu.SemaphoreType.DMA((SENDS,)),
-            pltpu.SemaphoreType.DMA((10,)),
+            pltpu.SemaphoreType.DMA((8,)),
             pltpu.SemaphoreType.DMA((28,)),
         ],
         compiler_params=pltpu.CompilerParams(
             collective_id=0, has_side_effects=True, vmem_limit_bytes=67043328
         ),
-    )(rows, w_gate, w_up, w_down, s_gate, s_up, s_down)
-
-
-def local(tokens, grad_out, gates, expert_ids, w_gate, w_up, w_down, s_gate, s_up, s_down):
-    count, width = tokens.shape
-    nodes = lax.axis_size("node")
-    slots = 2 * count // nodes
-    places = jnp.arange(slots, dtype=jnp.int32)
-    pair = 2 * jnp.arange(nodes, dtype=jnp.int32)[None, :]
-    chosen = [expert_ids[:, :, None] == (pair + e)[:, None, :] for e in range(2)]
-    gate = gates.astype(F32)[:, :, None]
-    weight = [jnp.sum(jnp.where(c, gate, 0.0), axis=1) for c in chosen]
-    named = [jnp.any(c, axis=1) for c in chosen]
-    member = named[0] | named[1]
-    both = (named[0] & named[1]).astype(F32)
-    ranking = jnp.cumsum(member.astype(jnp.int32), axis=0) - 1
-    pick = (member[:, :, None] & (ranking[:, :, None] == places)).astype(BF16)
-    side = jnp.stack([weight[0], weight[1], both], axis=-1)
-    side = jnp.sum(pick.astype(F32)[..., None] * side[:, :, None, :], axis=0)
-    side = jnp.pad(side, ((0, 0), (0, 0), (0, UNIT - 3))).astype(BF16)
-    pieces = [
-        jnp.einsum("tns,td->nsd", pick, value, preferred_element_type=F32).astype(BF16)
-        for value in (tokens, grad_out)
-    ]
-    rows = jnp.concatenate([pieces[0], side, pieces[1]], axis=2)
-    rows = lax.all_to_all(rows, "node", split_axis=0, concat_axis=0, tiled=True)
-    rows = rows.reshape(2, ROWS, rows.shape[2])
-    ret, dwg, dwu, dwd, dsg, dsu, dsd = expert_layer(
-        rows, w_gate, w_up, w_down, s_gate, s_up, s_down
-    )
-    ret = ret.reshape(nodes, slots, ret.shape[2])
-    ret = lax.all_to_all(ret, "node", split_axis=0, concat_axis=0, tiled=True)
-    dx = jnp.einsum("tns,nsd->td", pick, ret[:, :, :width], preferred_element_type=F32)
-    score = ret[:, :, width : width + 2].astype(F32)
-    score = jnp.sum(pick.astype(F32)[..., None] * score[None], axis=2)
-    dgates = sum(
-        jnp.sum(jnp.where(chosen[e], score[:, None, :, e], 0.0), axis=2) for e in range(2)
-    )
-    return dx.astype(BF16), dgates, dwg, dwu, dwd, dsg, dsu, dsd
+    )(tokens, grad_out, gates, ids, w_gate, w_up, w_down, s_gate, s_up, s_down)
 
 
 def solution(mesh):
@@ -410,7 +527,7 @@
     routed = P("node", None, "local")
     shared = P(None, "local")
     return jax.shard_map(
-        local,
+        expert_layer,
         mesh=mesh,
         in_specs=(flat,) * 4 + (routed,) * 3 + (shared,) * 3,
         out_specs=(flat, flat) + (routed,) * 3 + (P("node", "local"),) * 3,

time: 185 us -> 168 us (0.908)
  Pallas kernels: 131 us -> 153 us
  blocking collectives: 19.9 us -> 0 us
  waiting for transfers between devices: 9.63 us -> 0 us
  starting transfers between devices: 3.48 us -> 0 us
  matrix products: 3.34 us -> 0 us
  other arithmetic: 3.17 us -> 0 us
    pallas_call x1, Pallas kernels: 131 us -> 153 us  [expert_layer(): pl.pallas_call(body, out_shape=(shape(tokens.shape, BF16), shape(gates.sh...]
    all_to_all x1 -> x0, blocking collectives: 19.9 us -> none  [local(): rows = lax.all_to_all(rows, 'node', split_axis=0, concat_axis=0, tiled=True)]
    all_to_all x1 -> x0, waiting for transfers between devices: 9.63 us -> none  [local(): ret = lax.all_to_all(ret, 'node', split_axis=0, concat_axis=0, tiled=True)]
    unnamed x42 -> x19, local copies, waits for them, and re-layouts: 8.51 us -> 12.8 us
    all_to_all x1 -> x0, starting transfers between devices: 3.48 us -> none  [local(): ret = lax.all_to_all(ret, 'node', split_axis=0, concat_axis=0, tiled=True)]
    dot_general x3 -> x0, matrix products: 3.34 us -> none  [the longest x2 2.38 us: local(): jnp.einsum('tns,td->nsd', pick, value, preferred_element_type=F32)]
    reshape x2 -> x0, local copies, waits for them, and re-layouts: 3.18 us -> none  [the longest x1 2.04 us: local(): ret = ret.reshape(nodes, slots, ret.shape[2])]
  transfers between devices with their start and end apart: 1 -> 0, of which waited for: 1 -> 0; matrix products, arithmetic and copies ran while one was open for 0% -> 0% of each run, Pallas kernels for 0% -> 0%
where the time goes in v2:
time: 168 us
  Pallas kernels  153 us (91%)
  local copies, waits for them, and re-layouts  14.1 us (8%)
    pallas_call x1, Pallas kernels, expert_layer(): pl.pallas_call(body, out_shape=(shape(tokens.shape, BF16), shape(gates.sh...  153 us
    unnamed x19, local copies, waits for them, and re-layouts  12.8 us

profile of v2, /device:TPU:0, one launch (start us, length us, event | category | flops | bytes accessed | tf_op | source)
XLA Modules:
  0.0 167.8 jit_solution(7407205285906946629)
XLA Ops:
  0.6 1.4 copy.18.gate_ref
  2.0 1.4 copy.19.id_ref
  3.3 153.0 %shard_map.161 = (bf16[16,7168]{1,0:T(8,128)(2,1)}, f32[16,3]{1,0:T(8,128)}, bf16[1,7168,128]{2,1,0:T(8,128)(2,1)}, bf16[1,7168,128]{2,1,0:T(8,128)(2,1)}, bf16[...) custom-call(bf16[16,7168]{1,0:T(8,128)(2,1)} %tok_ref.1, ...), custom_call_target="tpu_custom_call" | custom-call | tf_op jit(solution)/shard_map/pallas_call | solution.py:478
  156.3 1.3 copy.20
  157.7 1.6 copy.28
  159.3 0.0 copy-start.1
  159.3 3.0 %copy.29 = bf16[1,7168,128]{2,1,0:T(8,128)(2,1)} copy(bf16[1,7168,128]{2,1,0:T(8,128)(2,1)} %get-tuple-element.26) | data formatting | bytes 3670016
  162.3 0.0 copy-done.1
  162.3 0.0 copy-start
  162.3 1.2 copy.30
  163.6 0.9 copy-done
  164.5 0.0 copy-start.4
  164.5 0.0 copy-start.3
  164.5 0.0 copy-start.2
  164.5 1.2 copy.31
  165.7 0.0 copy-done.4
  165.7 0.7 copy.32
  166.4 0.0 copy-done.3
  166.4 0.7 copy.33
  167.1 0.0 copy-done.2
  167.1 0.7 copy.34
Async XLA Ops:
  159.3 3.0 %copy-start.1 = (bf16[1,7168,128]{2,1,0:T(8,128)(2,1)S(1)}, bf16[1,7168,128]{2,1,0:T(8,128)(2,1)}, u32[]{:S(2)}) copy-start(bf16[1,7168,128]{2,1,0:T(8,128)(2,1)} %get-tuple-element.27) | copy-start | bytes 5505028
  162.3 2.2 %copy-start = (bf16[1,7168,128]{2,1,0:T(8,128)(2,1)S(1)}, bf16[1,7168,128]{2,1,0:T(8,128)(2,1)}, u32[]{:S(2)}) copy-start(bf16[1,7168,128]{2,1,0:T(8,128)(2,1)} %get-tuple-element.28) | copy-start | bytes 5505028
  164.5 1.2 copy-start.4
  164.5 1.9 %copy-start.3 = (bf16[896,128]{1,0:T(8,128)(2,1)S(1)}, bf16[896,128]{1,0:T(8,128)(2,1)}, u32[]{:S(2)}) copy-start(bf16[896,128]{1,0:T(8,128)(2,1)} %get-tuple-element.30) | copy-start | bytes 688132
  164.5 2.6 %copy-start.2 = (bf16[896,128]{1,0:T(8,128)(2,1)S(1)}, bf16[896,128]{1,0:T(8,128)(2,1)}, u32[]{:S(2)}) copy-start(bf16[896,128]{1,0:T(8,128)(2,1)} %get-tuple-element.31) | copy-start | bytes 688132

commit v3 on v2

--- a/solution.py
+++ b/solution.py
@@ -65,22 +65,12 @@
         pl.semaphore_signal(barrier, inc=1, device_id=device, device_id_type=MESH)
 
     count = ROWS
-    eye = lax.broadcasted_iota(jnp.int32, (count, count), 0) == lax.broadcasted_iota(
-        jnp.int32, (count, count), 1
-    )
-
-    def as_row(column):
-        return jnp.sum(jnp.where(eye, column, 0.0), axis=0, keepdims=True)
-
-    def as_column(row):
-        return jnp.sum(jnp.where(eye, row, 0.0), axis=1, keepdims=True)
-
     slot_row = lax.broadcasted_iota(jnp.int32, (2 * ROWS, count), 0)
     slot_node = ((z + (slot_row >> 3)) & 3) * 2 + ((core + (slot_row >> 2)) & 1)
     ids = id_ref[...].astype(F32)
     gates = gate_ref[...].astype(F32)
-    id_rows = [as_row(ids[:, k : k + 1]) for k in range(3)]
-    gate_rows = [as_row(gates[:, k : k + 1]) for k in range(3)]
+    id_rows = [ids[k : k + 1] for k in range(3)]
+    gate_rows = [gates[k : k + 1] for k in range(3)]
     names = [
         [(id_rows[k] == (2 * slot_node + e).astype(F32)).astype(F32) for k in range(3)]
         for e in range(2)
@@ -454,15 +444,37 @@
     store(given.at[0], dx_ref)
     score = answers(width, UNIT)
     for k in range(3):
-        row = jnp.sum(
+        dgate_ref[k : k + 1] = jnp.sum(
             pick * (names[0][k] * score[:, 0:1] + names[1][k] * score[:, 1:2]),
             axis=0, keepdims=True,
         )
-        dgate_ref[:, k : k + 1] = as_column(row)
     for copy in sends:
         copy.wait_send()
     for copy in stores:
         copy.wait()
+
+
+PIECES = 8
+
+
+def hand_on(*refs):
+    ins, outs, held, sems = refs[:8], refs[8:16], refs[16:24], refs[24]
+    copies = []
+    for i in (1, 2, 3, 4, 5, 6, 0, 7):
+        for p in range(PIECES if 1 <= i <= 3 else 1):
+            at = pl.ds(p * (held[i].shape[1] // PIECES), held[i].shape[1] // PIECES)
+            view = (lambda r, at=at: r.at[0, at]) if 1 <= i <= 3 else (lambda r: r)
+            pair = [
+                pltpu.make_async_copy(view(src), view(dst), sems.at[j, i * PIECES + p])
+                for j, (src, dst) in enumerate(((ins[i], held[i]), (held[i], outs[i])))
+            ]
+            pair[0].start()
+            copies.append(pair)
+    for pair in copies:
+        pair[0].wait()
+        pair[1].start()
+    for pair in copies:
+        pair[1].wait()
 
 
 SENDS = 103 + 9 + 9
@@ -475,11 +487,11 @@
     shape = jax.ShapeDtypeStruct
     anywhere = pl.BlockSpec(memory_space=pl.ANY)
     inside = pl.BlockSpec(memory_space=pltpu.VMEM)
-    return pl.pallas_call(
+    dx, dgates, *grads = pl.pallas_call(
         body,
         out_shape=(
             shape(tokens.shape, BF16),
-            shape(gates.shape, F32),
+            shape(gates.shape[::-1], F32),
             *(shape(w_gate.shape, BF16) for _ in range(3)),
             *(shape((block, UNIT), BF16) for _ in range(3)),
         ),
@@ -519,7 +531,20 @@
         compiler_params=pltpu.CompilerParams(
             collective_id=0, has_side_effects=True, vmem_limit_bytes=67043328
         ),
-    )(tokens, grad_out, gates, ids, w_gate, w_up, w_down, s_gate, s_up, s_down)
+    )(tokens, grad_out, gates.T, ids.T, w_gate, w_up, w_down, s_gate, s_up, s_down)
+    outs = (dx, *grads, dgates)
+    dx, *grads, dgates = pl.pallas_call(
+        hand_on,
+        out_shape=tuple(shape(o.shape, o.dtype) for o in outs),
+        in_specs=[anywhere] * 8,
+        out_specs=(anywhere,) * 8,
+        scratch_shapes=[
+            *(pltpu.VMEM(o.shape, o.dtype) for o in outs),
+            pltpu.SemaphoreType.DMA((2, 8 * PIECES)),
+        ],
+        compiler_params=pltpu.CompilerParams(vmem_limit_bytes=67043328),
+    )(*outs)
+    return (dx, dgates.T, *grads)
 
 
 def solution(mesh):

time: 168 us -> 160 us (0.952)
  local copies, waits for them, and re-layouts: 14.1 us -> 0 us
  Pallas kernels: 153 us -> 159 us
    unnamed x19 -> x0, local copies, waits for them, and re-layouts: 12.8 us -> none
    pallas_call x0 -> x1, Pallas kernels: none -> 6.28 us  [expert_layer(): pl.pallas_call(hand_on, out_shape=tuple((shape(o.shape, o.dtype) for o in...]
where the time goes in v3:
time: 160 us
  Pallas kernels  159 us (99%)
    pallas_call x1, Pallas kernels, expert_layer(): pl.pallas_call(body, out_shape=(shape(tokens.shape, BF16), shape(gates.sh...  153 us
    pallas_call x1, Pallas kernels, expert_layer(): pl.pallas_call(hand_on, out_shape=tuple((shape(o.shape, o.dtype) for o in...  6.28 us

profile of v3, /device:TPU:0, one launch (start us, length us, event | category | flops | bytes accessed | tf_op | source)
XLA Modules:
  0.0 160.0 jit_solution(1021758032243012778)
XLA Ops:
  0.6 153.0 %shard_map.161 = (bf16[16,7168]{1,0:T(8,128)(2,1)}, f32[3,16]{1,0:T(4,128)}, bf16[1,7168,128]{2,1,0:T(8,128)(2,1)}, bf16[1,7168,128]{2,1,0:T(8,128)(2,1)}, bf16[...) custom-call(bf16[16,7168]{1,0:T(8,128)(2,1)} %tok_ref.1, ...), custom_call_target="tpu_custom_call" | custom-call | tf_op jit(solution)/shard_map/pallas_call | solution.py:490
  153.7 6.3 %shard_map.162 = (bf16[16,7168]{1,0:T(8,128)(2,1)}, bf16[1,7168,128]{2,1,0:T(8,128)(2,1)}, bf16[1,7168,128]{2,1,0:T(8,128)(2,1)}, bf16[1,7168,128]{2,1,0:T(8,128...) custom-call(bf16[16,7168]{1,0:T(8,128)(2,1)} %get-tuple-element.24.ref, ...), custom_call_target="tpu_custom_call" | custom-call | tf_op jit(solution)/shard_map/pallas_call | solution.py:536

commit v4 on v3

--- a/solution.py
+++ b/solution.py
@@ -21,8 +21,8 @@
     tok_ref, grad_ref, gate_ref, id_ref, wg_ref, wu_ref, wd_ref, sg_ref, su_ref, sd_ref,
     dx_ref, dgate_ref, dwg_ref, dwu_ref, dwd_ref, dsg_ref, dsu_ref, dsd_ref,
     given, outgo, income, relay, answer, reply, relay_back, tt, tg, xx, w_all, v_all, gg, acc_p, acc_u,
-    r1, r2, q1, q2, sw, pw, z1, z2, dw, ds,
-    send_sem, recv_sem, load_sem, store_sem,
+    r1, r2, q1, q2, sw, pw, z1, z2,
+    send_sem, recv_sem, load_sem,
 ):
     width = wg_ref.shape[1]
     wide = width + UNIT
@@ -53,11 +53,6 @@
 
     load(tok_ref, given.at[0])
     load(grad_ref, given.at[1])
-    for i, ref in enumerate((wg_ref.at[0], wu_ref.at[0], sg_ref, su_ref)):
-        load(ref, w_all.at[:, pl.ds(i * UNIT, UNIT)])
-    for i, ref in enumerate((wd_ref.at[0], sd_ref)):
-        load(ref, v_all.at[:, pl.ds(i * UNIT, UNIT)])
-
     barrier = pltpu.get_barrier_semaphore()
     for device in (
         x_plus, x_minus, y_plus, y_minus, z_plus, z_minus, z_plus_other, z_minus_other, partner
@@ -130,6 +125,11 @@
         (2, 1): send(outgo.at[5], relay.at[1], z_minus),
         (1, 1): send(outgo.at[3], income.at[7], z_plus_other),
     }
+
+    for i, ref in enumerate((wg_ref.at[0], wu_ref.at[0], sg_ref, su_ref)):
+        load(ref, w_all.at[:, pl.ds(i * UNIT, UNIT)])
+    for i, ref in enumerate((wd_ref.at[0], sd_ref)):
+        load(ref, v_all.at[:, pl.ds(i * UNIT, UNIT)])
 
     def stack(h):
         def piece(at, size):
@@ -293,13 +293,6 @@
             back[h, "p", j] = send(xx.at[h, 2, upper[j]], r1.at[h, 0, j], plus)
             back[h, "m", j] = send(xx.at[h, 2, lower[j]], r1.at[h, 1, j], minus)
 
-    stores = []
-
-    def store(src, dst):
-        copy = pltpu.make_async_copy(src, dst, store_sem.at[len(stores)])
-        copy.start()
-        stores.append(copy)
-
     everything = 2 * RING * RING * ROWS
 
     def weights(parity):
@@ -310,9 +303,9 @@
             g = tg[:, :, :, :, at].reshape(everything, block)
             a = dot(t, gg[:, :, :, :, : 4 * UNIT].reshape(everything, 4 * UNIT), 0, 0)
             c = dot(g, gg[:, :, :, :, 4 * UNIT :].reshape(everything, 2 * UNIT), 0, 0)
-            dw[0, b] = a[:, :UNIT].astype(BF16)
-            dw[1, b] = a[:, UNIT : 2 * UNIT].astype(BF16)
-            dw[2, b] = c[:, :UNIT].astype(BF16)
+            dwg_ref[0, at] = a[:, :UNIT].astype(BF16)
+            dwu_ref[0, at] = a[:, UNIT : 2 * UNIT].astype(BF16)
+            dwd_ref[0, at] = c[:, :UNIT].astype(BF16)
             sw[parity, k, :, : 2 * UNIT] = a[:, 2 * UNIT :].astype(BF16)
             sw[parity, k, :, 2 * UNIT :] = c[:, UNIT:].astype(BF16)
             return carry
@@ -337,9 +330,6 @@
             add(xx.at[h, 3, lower[j]], r1.at[h, 1, j])
             full[h, "m", lower[j]] = send(xx.at[h, 3, lower[j]], r2.at[h, 1, lower[j]], minus)
     weights(core)
-    for b in range(8):
-        for j, ref in enumerate((dwg_ref, dwu_ref, dwd_ref)):
-            store(dw.at[j, b], ref.at[0, pl.ds(b * block, block)])
     swap.wait_recv()
 
     def add_swap(k, carry):
@@ -420,8 +410,7 @@
         copy.wait_recv()
     total = sw[core, z].astype(F32) + z2[0].astype(F32) + z2[1].astype(F32)
     for j, ref in enumerate((dsg_ref, dsu_ref, dsd_ref)):
-        ds[j] = total[:, j * UNIT : (j + 1) * UNIT].astype(BF16)
-        store(ds.at[j], ref)
+        ref[...] = total[:, j * UNIT : (j + 1) * UNIT].astype(BF16)
     home[3].wait_recv()
     home.append(send(relay_back.at[0], reply.at[4], z_plus))
     home[4].wait_recv()
@@ -437,11 +426,10 @@
     def finish(k, carry):
         at = pl.multiple_of(k * stretch, UNIT)
         total = dot(pick_bf16, answers(at, stretch).astype(BF16), 0, 0)
-        given[0, :, pl.ds(at, stretch)] = total.astype(BF16)
+        dx_ref[:, pl.ds(at, stretch)] = total.astype(BF16)
         return carry
 
     lax.fori_loop(0, 7, finish, 0)
-    store(given.at[0], dx_ref)
     score = answers(width, UNIT)
     for k in range(3):
         dgate_ref[k : k + 1] = jnp.sum(
@@ -450,31 +438,15 @@
         )
     for copy in sends:
         copy.wait_send()
-    for copy in stores:
+
+
+def hand_on(*refs):
+    ins, outs, sems = refs[:8], refs[8:16], refs[16]
+    copies = [pltpu.make_async_copy(*pair, sems.at[i]) for i, pair in enumerate(zip(ins, outs))]
+    for copy in copies:
+        copy.start()
+    for copy in copies:
         copy.wait()
-
-
-PIECES = 8
-
-
-def hand_on(*refs):
-    ins, outs, held, sems = refs[:8], refs[8:16], refs[16:24], refs[24]
-    copies = []
-    for i in (1, 2, 3, 4, 5, 6, 0, 7):
-        for p in range(PIECES if 1 <= i <= 3 else 1):
-            at = pl.ds(p * (held[i].shape[1] // PIECES), held[i].shape[1] // PIECES)
-            view = (lambda r, at=at: r.at[0, at]) if 1 <= i <= 3 else (lambda r: r)
-            pair = [
-                pltpu.make_async_copy(view(src), view(dst), sems.at[j, i * PIECES + p])
-                for j, (src, dst) in enumerate(((ins[i], held[i]), (held[i], outs[i])))
-            ]
-            pair[0].start()
-            copies.append(pair)
-    for pair in copies:
-        pair[0].wait()
-        pair[1].start()
-    for pair in copies:
-        pair[1].wait()
 
 
 SENDS = 103 + 9 + 9
@@ -490,13 +462,13 @@
     dx, dgates, *grads = pl.pallas_call(
         body,
         out_shape=(
-            shape(tokens.shape, BF16),
-            shape(gates.shape[::-1], F32),
-            *(shape(w_gate.shape, BF16) for _ in range(3)),
-            *(shape((block, UNIT), BF16) for _ in range(3)),
+            pltpu.VMEM(tokens.shape, BF16),
+            pltpu.VMEM(gates.shape[::-1], F32),
+            *(pltpu.VMEM(w_gate.shape, BF16) for _ in range(3)),
+            *(pltpu.VMEM((block, UNIT), BF16) for _ in range(3)),
         ),
         in_specs=[anywhere] * 2 + [inside] * 2 + [anywhere] * 6,
-        out_specs=(anywhere, inside) + (anywhere,) * 6,
+        out_specs=(inside,) * 8,
         scratch_shapes=[
             pltpu.VMEM((2, ROWS, width), BF16),
             pltpu.VMEM((8, 4, wide + width), BF16),
@@ -521,28 +493,22 @@
             pltpu.VMEM((RING, block, 3 * UNIT), BF16),
             pltpu.VMEM((2, block // 2, 3 * UNIT), BF16),
             pltpu.VMEM((2, block, 3 * UNIT), BF16),
-            pltpu.VMEM((3, 8, block, UNIT), BF16),
-            pltpu.VMEM((3, block, UNIT), BF16),
             pltpu.SemaphoreType.DMA((SENDS,)),
             pltpu.SemaphoreType.DMA((SENDS,)),
             pltpu.SemaphoreType.DMA((8,)),
-            pltpu.SemaphoreType.DMA((28,)),
         ],
         compiler_params=pltpu.CompilerParams(
-            collective_id=0, has_side_effects=True, vmem_limit_bytes=67043328
+            collective_id=0, has_side_effects=True, vmem_limit_bytes=60500000
         ),
     )(tokens, grad_out, gates.T, ids.T, w_gate, w_up, w_down, s_gate, s_up, s_down)
     outs = (dx, *grads, dgates)
     dx, *grads, dgates = pl.pallas_call(
         hand_on,
         out_shape=tuple(shape(o.shape, o.dtype) for o in outs),
-        in_specs=[anywhere] * 8,
+        in_specs=[inside] * 8,
         out_specs=(anywhere,) * 8,
-        scratch_shapes=[
-            *(pltpu.VMEM(o.shape, o.dtype) for o in outs),
-            pltpu.SemaphoreType.DMA((2, 8 * PIECES)),
-        ],
-        compiler_params=pltpu.CompilerParams(vmem_limit_bytes=67043328),
+        scratch_shapes=[pltpu.SemaphoreType.DMA((8,))],
+        compiler_params=pltpu.CompilerParams(vmem_limit_bytes=8 * 2**20),
     )(*outs)
     return (dx, dgates.T, *grads)
 

time: 160 us -> 155 us (0.969)
  Pallas kernels: 159 us -> 154 us
    pallas_call x1, Pallas kernels: 6.28 us -> 2.79 us  [expert_layer(): pl.pallas_call(hand_on, out_shape=tuple((shape(o.shape, o.dtype) for o in...]
where the time goes in v4:
time: 155 us
  Pallas kernels  154 us (99%)
    pallas_call x1, Pallas kernels, expert_layer(): pl.pallas_call(body, out_shape=(pltpu.VMEM(tokens.shape, BF16), pltpu.VME...  152 us

profile of v4, /device:TPU:0, one launch (start us, length us, event | category | flops | bytes accessed | tf_op | source)
XLA Modules:
  0.0 155.1 jit_solution(210927297514185757)
XLA Ops:
  0.6 151.7 %shard_map.161 = (bf16[16,7168]{1,0:T(8,128)(2,1)S(1)}, f32[3,16]{1,0:T(4,128)S(1)}, bf16[1,7168,128]{2,1,0:T(8,128)(2,1)S(1)}, bf16[1,7168,128]{2,1,0:T(8,128)(...) custom-call(bf16[16,7168]{1,0:T(8,128)(2,1)} %tok_ref.1, ...), custom_call_target="tpu_custom_call" | custom-call | tf_op jit(solution)/shard_map/pallas_call | solution.py:462
  152.3 2.8 %shard_map.162 = (bf16[16,7168]{1,0:T(8,128)(2,1)}, bf16[1,7168,128]{2,1,0:T(8,128)(2,1)}, bf16[1,7168,128]{2,1,0:T(8,128)(2,1)}, bf16[1,7168,128]{2,1,0:T(8,128...) custom-call(bf16[16,7168]{1,0:T(8,128)(2,1)S(1)} %get-tuple-element.24, ...), custom_call_target="tpu_custom_call" | custom-call | tf_op jit(solution)/shard_map/pallas_call | solution.py:505

commit v5 on v4

--- a/solution.py
+++ b/solution.py
@@ -119,12 +119,13 @@
     across = {
         (0, 1): send(outgo.at[1], income.at[1], partner),
         (3, 0): send(outgo.at[6], income.at[2], z_minus),
+        (1, 0): send(outgo.at[2], income.at[6], z_plus),
         (2, 0): send(outgo.at[4], relay.at[0], z_plus),
+        (2, 1): send(outgo.at[5], relay.at[1], z_minus),
         (3, 1): send(outgo.at[7], income.at[3], z_minus_other),
-        (1, 0): send(outgo.at[2], income.at[6], z_plus),
-        (2, 1): send(outgo.at[5], relay.at[1], z_minus),
         (1, 1): send(outgo.at[3], income.at[7], z_plus_other),
     }
+    slots = ((0, 1, 2, 6), (4, 5, 3, 7))
 
     for i, ref in enumerate((wg_ref.at[0], wu_ref.at[0], sg_ref, su_ref)):
         load(ref, w_all.at[:, pl.ds(i * UNIT, UNIT)])
@@ -135,8 +136,8 @@
         def piece(at, size):
             return jnp.concatenate(
                 [
-                    (outgo if h == 0 and s == 0 else income)[4 * h + s, :, pl.ds(at, size)].astype(F32)
-                    for s in range(4)
+                    (income if s else outgo)[s, :, pl.ds(at, size)].astype(F32)
+                    for s in slots[h]
                 ],
                 0,
             ).astype(BF16)
@@ -158,12 +159,12 @@
             one[h, "p", part] = send(a.at[h, 0, 0], a.at[h, 0, 3], plus)
             one[h, "m", part] = send(b.at[h, 0, 0], b.at[h, 0, 1], minus)
 
-    across[2, 0].wait_recv()
-    forth = [send(relay.at[0], income.at[4], z_plus)]
-    for key in ((0, 1), (3, 0), (3, 1)):
+    for key in ((0, 1), (3, 0), (1, 0)):
         across[key].wait_recv()
     stack(0)
     first_hop(0)
+    across[2, 0].wait_recv()
+    forth = [send(relay.at[0], income.at[4], z_plus)]
     across[2, 1].wait_recv()
     forth.append(send(relay.at[1], income.at[5], z_minus_other))
 
@@ -182,7 +183,7 @@
         far[h, "m"] = send(tg.at[h, 0, 1], tg.at[h, 0, 2], minus)
 
     second_hop(0, 0)
-    for copy in (across[1, 0], across[1, 1], *forth):
+    for copy in (across[3, 1], across[1, 1], *forth):
         copy.wait_recv()
     stack(1)
     first_hop(1)
@@ -389,21 +390,21 @@
             for i in range(2):
                 total = total + q2[h, i, :, at].astype(F32)
             for s in range(4):
-                answer[4 * h + s, :, at] = total[4 * s : 4 * s + 4].astype(BF16)
+                answer[slots[h][s], :, at] = total[4 * s : 4 * s + 4].astype(BF16)
             return carry
 
         lax.fori_loop(0, wide // (3 * UNIT), one_stretch, 0)
         if h == 0:
             home = [
                 send(answer.at[2], reply.at[6], z_plus),
-                send(answer.at[3], reply.at[7], z_plus_other),
+                send(answer.at[6], reply.at[2], z_minus),
                 send(answer.at[1], reply.at[1], partner),
             ]
         else:
             home += [
                 send(answer.at[4], relay_back.at[0], z_plus),
                 send(answer.at[5], relay_back.at[1], z_minus),
-                send(answer.at[6], reply.at[2], z_minus),
+                send(answer.at[3], reply.at[7], z_plus_other),
                 send(answer.at[7], reply.at[3], z_minus_other),
             ]
     for copy in z_full:

time: 155 us -> 152 us (0.981); the launches traced: 155 us -> 150 us
  Pallas kernels: 154 us -> 150 us
    pallas_call x1, Pallas kernels: 152 us -> 147 us  [expert_layer(): pl.pallas_call(body, out_shape=(pltpu.VMEM(tokens.shape, BF16), pltpu.VME...]
where the time goes in v5:
time: 152 us; the launch traced here: 150 us
  Pallas kernels  150 us (99%)
    pallas_call x1, Pallas kernels, expert_layer(): pl.pallas_call(body, out_shape=(pltpu.VMEM(tokens.shape, BF16), pltpu.VME...  147 us

profile of v5, /device:TPU:0, one launch (start us, length us, event | category | flops | bytes accessed | tf_op | source)
XLA Modules:
  0.0 150.5 jit_solution(16619109239697365683)
XLA Ops:
  0.6 147.0 %shard_map.161 = (bf16[16,7168]{1,0:T(8,128)(2,1)S(1)}, f32[3,16]{1,0:T(4,128)S(1)}, bf16[1,7168,128]{2,1,0:T(8,128)(2,1)S(1)}, bf16[1,7168,128]{2,1,0:T(8,128)(...) custom-call(bf16[16,7168]{1,0:T(8,128)(2,1)} %tok_ref.1, ...), custom_call_target="tpu_custom_call" | custom-call | tf_op jit(solution)/shard_map/pallas_call | solution.py:463
  147.7 2.8 %shard_map.162 = (bf16[16,7168]{1,0:T(8,128)(2,1)}, bf16[1,7168,128]{2,1,0:T(8,128)(2,1)}, bf16[1,7168,128]{2,1,0:T(8,128)(2,1)}, bf16[1,7168,128]{2,1,0:T(8,128...) custom-call(bf16[16,7168]{1,0:T(8,128)(2,1)S(1)} %get-tuple-element.24, ...), custom_call_target="tpu_custom_call" | custom-call | tf_op jit(solution)/shard_map/pallas_call | solution.py:506
